TPU v7x, 8 devices: a whole 2x2x1 slice. The times are simulated.
8 devices in a mesh: rep: 1 (over z), data: 2 (over y), model: 4 (over x, core).
Axes of the slice: x: 2, y: 2, z: 1, core: 2. Of those that a mesh axis runs over, the one named last changes fastest.
Arguments:
- x: bfloat16 [4, 2048, 2048], P(('rep', 'data'), 'model')
- lengths: int32 [4], P(('rep', 'data'))
- gamma: bfloat16 [2, 2048], P(None, 'data')
- w_in: bfloat16 [2, 2048, 34816], P(None, 'data', 'model')
- w_kv: bfloat16 [2, 2048, 512], P(None, 'data')
- w_out: bfloat16 [2, 18432, 2048], P(None, 'model', 'data')
Outputs:
- output: bfloat16 [4, 2048, 2048], P(('rep', 'data'), 'model')
All inputs are finite; a program needn't handle non-finite values.
Results may differ from a plain program's by a relative error of at most 0.0141291.
Values are sent between devices in bfloat16 or wider.
A program may use at most 1 GiB of HBM per device.

v0:
```python
import jax
import jax.numpy as jnp
from jax import lax
from jax.sharding import PartitionSpec as P

EPSILON = 1e-6


def rms_norm(x_in, gain):
    x_f32 = x_in.astype(jnp.float32)
    inv_rms = lax.rsqrt(jnp.mean(x_f32 * x_f32, axis=-1, keepdims=True) + EPSILON)
    return (x_f32 * inv_rms * gain.astype(jnp.float32)).astype(jnp.bfloat16)


def attend(queries, keys, values, seq_lens, q_offset, block_len):
    n_batch, n_query, n_heads, head_dim = queries.shape
    n_blocks = n_query // block_len
    q_blocks = queries.reshape(n_batch, n_blocks, block_len, n_heads, head_dim)
    key_pos = jnp.arange(keys.shape[1])

    def one_block(blk_idx):
        q_blk = lax.dynamic_index_in_dim(q_blocks, blk_idx, axis=1, keepdims=False)
        scores = jnp.einsum("crie,cle->cirl", q_blk, keys, preferred_element_type=jnp.float32) * (head_dim ** -0.5)
        q_pos = q_offset + blk_idx * block_len + jnp.arange(block_len)
        visible = (key_pos[None, None, :] <= q_pos[None, :, None]) & (key_pos[None, None, :] < seq_lens[:, None, None])
        scores = jnp.where(visible[:, None], scores, -1e30)
        attn_probs = jax.nn.softmax(scores, axis=-1).astype(jnp.bfloat16)
        blk_out = jnp.einsum("cirl,cle->crie", attn_probs, values, preferred_element_type=jnp.float32)
        return blk_out.astype(jnp.bfloat16).reshape(n_batch, block_len, n_heads * head_dim)

    return lax.map(one_block, jnp.arange(n_blocks))


def solution(mesh):
    batch_axes = ("rep", "data")

    def local_step(x_loc, lens_loc, gamma_loc, w_in_loc, w_kv_loc, w_out_loc):
        n_batch, seq_loc, d_model = x_loc.shape
        head_dim = w_kv_loc.shape[2] // 2
        in_local = w_in_loc.shape[2]
        out_local = w_out_loc.shape[1]
        ff_local = in_local - out_local
        attn_cols = out_local - ff_local
        hidden = x_loc
        for layer in range(gamma_loc.shape[0]):
            gain = lax.all_gather(gamma_loc[layer], "data", axis=0, tiled=True)
            w_in_full = lax.all_gather(w_in_loc[layer], "data", axis=0, tiled=True)
            w_kv_full = lax.all_gather(w_kv_loc[layer], "data", axis=0, tiled=True)
            w_out_full = lax.all_gather(w_out_loc[layer], "data", axis=1, tiled=True)
            normed = rms_norm(hidden, gain)
            h_full = lax.all_gather(normed, "model", axis=1, tiled=True)
            seq_len = h_full.shape[1]
            projected = jnp.einsum("btd,dc->btc", h_full, w_in_full, preferred_element_type=jnp.float32).astype(jnp.bfloat16)
            key_value = jnp.einsum("btd,de->bte", h_full, w_kv_full, preferred_element_type=jnp.float32).astype(jnp.bfloat16)
            queries = projected[:, :, :attn_cols].reshape(n_batch, seq_len, attn_cols // head_dim, head_dim)
            attn_blocks = attend(queries, key_value[:, :, :head_dim], key_value[:, :, head_dim:], lens_loc, 0, seq_loc)
            gate = projected[:, :, attn_cols:attn_cols + ff_local].astype(jnp.float32)
            up_proj = projected[:, :, attn_cols + ff_local:].astype(jnp.float32)
            mlp_out = (jax.nn.silu(gate) * up_proj).astype(jnp.bfloat16)
            z_attn = jnp.einsum("nbqe,ed->bnqd", attn_blocks, w_out_full[:attn_cols], preferred_element_type=jnp.float32).reshape(n_batch, seq_len, d_model)
            z_mlp = jnp.einsum("btf,fd->btd", mlp_out, w_out_full[attn_cols:], preferred_element_type=jnp.float32)
            z_part = (z_attn + z_mlp).astype(jnp.bfloat16)
            z_sum = lax.psum_scatter(z_part, "model", scatter_dimension=1, tiled=True)
            hidden = (hidden.astype(jnp.float32) + z_sum.astype(jnp.float32)).astype(jnp.bfloat16)
        return hidden

    in_specs = (
        P(batch_axes, "model", None),
        P(batch_axes),
        P(None, "data"),
        P(None, "data", "model"),
        P(None, "data", None),
        P(None, "model", "data"),
    )
    return jax.shard_map(local_step, mesh=mesh, in_specs=in_specs, out_specs=P(batch_axes, "model", None), check_vma=False)
```

profile of v0, /device:TPU:0, one launch (start us, length us, event | category | flops | bytes accessed | tf_op | source)
XLA Modules:
  0.0 2326.1 jit_solution(10208923564774465019)
XLA Ops:
  25.0 25.8 %fusion.74 = (bf16[1,1024,8704]{2,1,0:T(8,128)(2,1)}, bf16[1,1024,8704]{2,1,0:T(8,128)(2,1)}) fusion(bf16[2,1024,8704]{2,1,0:T(8,128)(2,1)} %param.13), kind=kLoop, calls=%fused_computation.104 | loop fusion | bytes 71303168 | tf_op jit(solution)/shard_map/slice | solution.py:47
  65.9 82.5 %all-gather.17.cloned.1.call-done = bf16[2,2048,2048]{2,1,0:T(8,128)(2,1)} async-done(((bf16[2,512,2048]{2,1,0:T(8,128)(2,1)}), bf16[2,2048,2048]{2,1,0:T(8,128)(2,1)}) %all-gather.17.cloned.1.call-update) | async-done | bytes 16777232 | tf_op jit(solution)/shard_map/all_gather | solution.py:51
  165.6 395.2 %all-gather.21.cloned.1.call-done = bf16[1,2048,8704]{2,1,0:T(8,128)(2,1)} async-done(((bf16[1,1024,8704]{2,1,0:T(8,128)(2,1)}), bf16[1,2048,8704]{2,1,0:T(8,128)(2,1)}) %all-gather.21.cloned.1.call-update) | async-done | bytes 35651600 | tf_op jit(solution)/shard_map/all_gather | solution.py:47
  560.8 160.2 %convolution_convert_fusion.1 = bf16[2,2048,8704]{2,1,0:T(8,128)(2,1)} fusion(bf16[2,2048,2048]{2,1,0:T(8,128)(2,1)} %all-gather.17.cloned.1.call-done, bf16[1,2048,8704]{2,1,0:T(8,128)(2,1)} %all-gather.21.cloned.1.call-done), kind=kOutput, calls=%fused_computation.65 | convolution fusion | flops 146064539648 | bytes 123731968 | tf_op jit(solution)/shard_map/btd,dc->btc/dot_general | solution.py:53
  734.9 182.4 %while.24 = (s32[]{:T(128)}, bf16[4,2,512,512]{2,3,1,0:T(8,128)(2,1)}, s32[4]{0:T(128)S(1)}, s32[2]{0:T(128)S(1)}, bf16[2,4,512,2,256]{4,3,2,1,0:T(2,128)(2,1)},...) while((s32[]{:T(128)}, ...), condition=%wide.region_4.5_spmd.clone.clone, body=%wide.region_1.4_spmd.clone.clone.sunk | while | flops 4332198400 | bytes 83915448 | solution.py:31
  750.4 20.4 fusion.102
  796.0 20.4 fusion.102
  841.5 20.4 fusion.102
  887.0 20.4 fusion.102
  917.3 18.3 convolution_bitcast_fusion.1
  935.6 23.0 copy.10
  958.6 89.1 %fusion.51 = bf16[2,2048,2048]{2,1,0:T(8,128)(2,1)} fusion(f32[2,4,512,2048]{3,2,1,0:T(8,128)} %copy.10, bf16[1,4608,2048]{2,1,0:T(8,128)(2,1)} %all-gather.25.cloned.1.call-done, bf16[2,2048,8704]{2,1,0:T(8,128)(2,1)} %convolution_convert_fusion.1), kind=kOutput, calls=%fused_computation.71 | convolution fusion | flops 68870471680 | bytes 134217728 | tf_op jit(solution)/shard_map/btf,fd->btd/dot_general | solution.py:61
  1052.8 113.8 %reduce-scatter.3.cloned.1.call-done = bf16[2,512,2048]{2,1,0:T(8,128)(2,1)} async-done(((bf16[2,2048,2048]{2,1,0:T(8,128)(2,1)}), bf16[2,512,2048]{2,1,0:T(8,128)(2,1)}) %reduce-scatter.3.cloned.1.call-update) | async-done | bytes 4194320 | tf_op jit(solution)/shard_map/reduce_scatter | solution.py:63
  1177.9 401.0 %all-gather.27.cloned.1.call-done = bf16[1,2048,8704]{2,1,0:T(8,128)(2,1)} async-done(((bf16[1,1024,8704]{2,1,0:T(8,128)(2,1)}), bf16[1,2048,8704]{2,1,0:T(8,128)(2,1)}) %all-gather.27.cloned.1.call-update) | async-done | bytes 35651600 | tf_op jit(solution)/shard_map/all_gather | solution.py:47
  1578.8 105.7 %all-gather.19.cloned.1.call-done = bf16[2,2048,2048]{2,1,0:T(8,128)(2,1)} async-done(((bf16[2,512,2048]{2,1,0:T(8,128)(2,1)}), bf16[2,2048,2048]{2,1,0:T(8,128)(2,1)}) %all-gather.19.cloned.1.call-update) | async-done | bytes 16777232 | tf_op jit(solution)/shard_map/all_gather | solution.py:51
  1684.6 160.1 %convolution_convert_fusion = bf16[2,2048,8704]{2,1,0:T(8,128)(2,1)} fusion(bf16[2,2048,2048]{2,1,0:T(8,128)(2,1)} %all-gather.19.cloned.1.call-done, bf16[1,2048,8704]{2,1,0:T(8,128)(2,1)} %all-gather.27.cloned.1.call-done), kind=kOutput, calls=%fused_computation.64 | convolution fusion | flops 146064539648 | bytes 123731968 | tf_op jit(solution)/shard_map/btd,dc->btc/dot_general | solution.py:53
  1877.2 182.3 %while.25 = (s32[]{:T(128)}, bf16[4,2,512,512]{2,3,1,0:T(8,128)(2,1)}, s32[4]{0:T(128)S(1)}, s32[2]{0:T(128)S(1)}, bf16[2,4,512,2,256]{4,3,2,1,0:T(2,128)(2,1)},...) while((s32[]{:T(128)}, ...), condition=%wide.region_10.11_spmd.clone.clone, body=%wide.region_7.10_spmd.clone.clone.sunk | while | flops 4332198400 | bytes 83915448 | solution.py:31
  1892.6 20.4 fusion.107
  1938.2 20.4 fusion.107
  1983.7 20.4 fusion.107
  2029.3 20.4 fusion.107
  2077.9 23.0 copy.14
  2100.9 89.3 %fusion.50 = bf16[2,2048,2048]{2,1,0:T(8,128)(2,1)} fusion(f32[2,4,512,2048]{3,2,1,0:T(8,128)} %copy.14, bf16[1,4608,2048]{2,1,0:T(8,128)(2,1)} %all-gather.31.cloned.1.call-done, bf16[2,2048,8704]{2,1,0:T(8,128)(2,1)} %convolution_convert_fusion), kind=kOutput, calls=%fused_computation.69 | convolution fusion | flops 68870471680 | bytes 134217728 | tf_op jit(solution)/shard_map/btf,fd->btd/dot_general | solution.py:61
  2190.2 118.9 %reduce-scatter.5.cloned.1.call-done = bf16[2,512,2048]{2,1,0:T(8,128)(2,1)} async-done(((bf16[2,2048,2048]{2,1,0:T(8,128)(2,1)}), bf16[2,512,2048]{2,1,0:T(8,128)(2,1)}) %reduce-scatter.5.cloned.1.call-update) | async-done | bytes 4194320 | tf_op jit(solution)/shard_map/reduce_scatter | solution.py:63
  (137 shorter events, 322.5 us)
Async XLA Ops:
  6.5 59.3 %all-gather.23.cloned.1.call-start = ((), (), s32[]{:S(2)}) async-start(), calls=%async_computation.7 | async-start | bytes 3145728 | tf_op jit(solution)/shard_map/all_gather | solution.py:48
  9.5 138.9 %all-gather.17.cloned.1.call-start = ((), (), s32[]{:S(2)}) async-start(), calls=%async_computation.2 | async-start | bytes 20971520 | tf_op jit(solution)/shard_map/all_gather | solution.py:51
  25.0 535.8 %all-gather.21.cloned.1.call-start = ((), (), s32[]{:S(2)}) async-start(), calls=%async_computation.6 | async-start | bytes 53477376 | tf_op jit(solution)/shard_map/all_gather | solution.py:47
  50.9 866.4 %all-gather.25.cloned.1.call-start = ((), (), s32[]{:S(2)}) async-start(), calls=%async_computation.8 | async-start | bytes 28311552 | tf_op jit(solution)/shard_map/all_gather | solution.py:49
  65.8 1100.8 %reduce-scatter.3.cloned.1.call-start = ((), (), s32[]{:S(2)}) async-start(), calls=%async_computation.3 | async-start | bytes 20971520 | tf_op jit(solution)/shard_map/reduce_scatter | solution.py:63
  725.5 9.4 copy-start.1
  725.5 9.4 copy-start.3
  1047.7 531.1 %all-gather.27.cloned.1.call-start = ((), (), s32[]{:S(2)}) async-start(), calls=%async_computation.9 | async-start | bytes 53477376 | tf_op jit(solution)/shard_map/all_gather | solution.py:47
  1047.8 0.7 copy-start.5
  1048.3 636.3 %all-gather.19.cloned.1.call-start = ((), (), s32[]{:S(2)}) async-start(), calls=%async_computation.4 | async-start | bytes 20971520 | tf_op jit(solution)/shard_map/all_gather | solution.py:51
  1166.6 5.0 copy-start
  1166.6 5.9 copy-start.2
  1176.3 679.7 %all-gather.29.cloned.1.call-start = ((), (), s32[]{:S(2)}) async-start(), calls=%async_computation.10 | async-start | bytes 3145728 | tf_op jit(solution)/shard_map/all_gather | solution.py:48
  1177.1 882.5 %all-gather.31.cloned.1.call-start = ((), (), s32[]{:S(2)}) async-start(), calls=%async_computation.11 | async-start | bytes 28311552 | tf_op jit(solution)/shard_map/all_gather | solution.py:49
  1177.8 1131.3 %reduce-scatter.5.cloned.1.call-start = ((), (), s32[]{:S(2)}) async-start(), calls=%async_computation.5 | async-start | bytes 20971520 | tf_op jit(solution)/shard_map/reduce_scatter | solution.py:63
  1869.3 8.0 copy-start.4
Sparse Core Ops, SparseCore 0:
  9.7 32.9 all-gather.22
  44.2 104.1 all-gather.16
  150.0 410.7 all-gather.20
  562.2 221.9 all-gather.24
  1047.8 118.7 reduce-scatter.2
  1168.0 410.7 all-gather.26
  1580.3 104.1 all-gather.18
  1686.1 30.1 all-gather.28
  1717.8 221.9 all-gather.30
  2190.3 118.7 reduce-scatter.4
where the time goes:
time: 2330 us
  waiting for transfers between devices  1220 us (52%)
  matrix products  697 us (30%)
  other arithmetic  206 us (9%)
  local copies, waits for them, and re-layouts  158 us (7%)
    all_gather x2, waiting for transfers between devices, local_step(): w_in_full = lax.all_gather(w_in_loc[layer], 'data', axis=0, tiled=True)  796 us
    dot_general x2, matrix products, local_step(): jnp.einsum('btd,dc->btc', h_full, w_in_full, preferred_element_type=jnp.f...  320 us
    reduce_scatter x2, waiting for transfers between devices, local_step(): z_sum = lax.psum_scatter(z_part, 'model', scatter_dimension=1, tiled=True)  233 us
    all_gather x2, waiting for transfers between devices, local_step(): h_full = lax.all_gather(normed, 'model', axis=1, tiled=True)  188 us
    dot_general x2, matrix products, local_step(): jnp.einsum('btf,fd->btd', mlp_out, w_out_full[attn_cols:], preferred_elem...  178 us
    sub x8, other arithmetic, one_block(): attn_probs = jax.nn.softmax(scores, axis=-1).astype(jnp.bfloat16)  163 us
    dot_general x8, matrix products, one_block(): jnp.einsum('cirl,cle->crie', attn_probs, values, preferred_element_type=j...  70.5 us
    dot_general x8, matrix products, one_block(): jnp.einsum('crie,cle->cirl', q_blk, keys, preferred_element_type=jnp.floa...  65.3 us
  transfers between devices with their start and end apart: 10, of which 6 were waited for; matrix products, arithmetic and copies ran while one was open for 34% of the time, Pallas kernels for 0%

commit v1 on v0

v1 whole, which is shorter than its diff:
```python
import functools

import jax
import jax.numpy as jnp
from jax import lax
from jax.experimental import pallas as pl
from jax.experimental.pallas import tpu as pltpu
from jax.sharding import PartitionSpec as P

EPSILON = 1e-6
VMEM_LIMIT = 60 * 1024 * 1024
BF16 = jnp.bfloat16
F32 = jnp.float32


def rms_norm(x_in, gain):
    x_f32 = x_in.astype(F32)
    inv_rms = lax.rsqrt(jnp.mean(x_f32 * x_f32, axis=-1, keepdims=True) + EPSILON)
    return (x_f32 * inv_rms * gain.astype(F32)).astype(BF16)


def gated_kernel(idx_ref, h_ref, g_own, u_own, g_oth, u_oth, out_ref):
    half = g_own.shape[0]
    h_a = h_ref[:, :half]
    h_b = h_ref[:, half:]
    gate = jnp.dot(h_a, g_own[...], preferred_element_type=F32) + jnp.dot(h_b, g_oth[...], preferred_element_type=F32)
    up = jnp.dot(h_a, u_own[...], preferred_element_type=F32) + jnp.dot(h_b, u_oth[...], preferred_element_type=F32)
    gate = gate.astype(BF16).astype(F32)
    up = up.astype(BF16).astype(F32)
    out_ref[...] = (gate * jax.nn.sigmoid(gate) * up).astype(BF16)


def gated(h, w_own, w_oth, layer, idx, g_col, u_col, width, tile_m=1024, tile_n=512):
    rows, d_model = h.shape
    half = d_model // 2
    n_tiles = width // tile_n
    g_blk, u_blk = g_col // tile_n, u_col // tile_n
    return pl.pallas_call(
        gated_kernel,
        grid_spec=pltpu.PrefetchScalarGridSpec(
            num_scalar_prefetch=1,
            grid=(n_tiles, rows // tile_m),
            in_specs=[
                pl.BlockSpec((tile_m, d_model), lambda n, m, s: (m, 0)),
                pl.BlockSpec((None, half, tile_n), lambda n, m, s: (layer, 0, g_blk + s[0] + n)),
                pl.BlockSpec((None, half, tile_n), lambda n, m, s: (layer, 0, u_blk + s[0] + n)),
                pl.BlockSpec((half, tile_n), lambda n, m, s: (0, n)),
                pl.BlockSpec((half, tile_n), lambda n, m, s: (0, n_tiles + n)),
            ],
            out_specs=pl.BlockSpec((tile_m, tile_n), lambda n, m, s: (m, n)),
        ),
        out_shape=jax.ShapeDtypeStruct((rows, width), BF16),
        compiler_params=pltpu.CompilerParams(vmem_limit_bytes=VMEM_LIMIT),
        cost_estimate=pl.CostEstimate(flops=4 * rows * d_model * width, bytes_accessed=2 * (rows * d_model * n_tiles + 2 * d_model * width + rows * width), transcendentals=rows * width),
        name="gated",
    )(idx, h, w_own, w_own, w_oth, w_oth)


def project_kernel(n_lhs, *refs):
    lhs, w_ref, out_ref = refs[:n_lhs], refs[n_lhs], refs[n_lhs + 1]
    row = 0
    acc = None
    for ref in lhs:
        part = jnp.dot(ref[...], w_ref[row:row + ref.shape[1], :], preferred_element_type=F32)
        acc = part if acc is None else acc + part
        row += ref.shape[1]
    out_ref[...] = acc.astype(BF16)


def project(lhs, weights, layer=None, tile_m=1024, tile_n=512):
    rows = lhs[0].shape[0]
    depth, cols = weights.shape[-2:]
    tile_n = min(tile_n, cols)
    if layer is None:
        w_spec = pl.BlockSpec((depth, tile_n), lambda n, m: (0, n))
    else:
        w_spec = pl.BlockSpec((None, depth, tile_n), lambda n, m: (layer, 0, n))
    return pl.pallas_call(
        functools.partial(project_kernel, len(lhs)),
        grid=(cols // tile_n, rows // tile_m),
        in_specs=[pl.BlockSpec((tile_m, a.shape[1]), lambda n, m: (m, 0)) for a in lhs] + [w_spec],
        out_specs=pl.BlockSpec((tile_m, tile_n), lambda n, m: (m, n)),
        out_shape=jax.ShapeDtypeStruct((rows, cols), BF16),
        compiler_params=pltpu.CompilerParams(vmem_limit_bytes=VMEM_LIMIT),
        cost_estimate=pl.CostEstimate(flops=2 * rows * depth * cols, bytes_accessed=2 * (rows * depth * (cols // tile_n) + depth * cols + rows * cols), transcendentals=0),
        name="project",
    )(*lhs, weights)


def attend_kernel(block, n_blocks, lens_ref, q_ref, k_ref, v_ref, out_ref):
    seq_len = lens_ref[pl.program_id(0)]
    which = pl.program_id(2)
    head_dim = q_ref.shape[1]
    for blk in range(n_blocks):
        @pl.when(which == blk)
        def _(blk=blk):
            keys = (blk + 1) * block
            scores = lax.dot_general(q_ref[...], k_ref[:keys, :], (((1,), (1,)), ((), ())), preferred_element_type=F32) * (head_dim ** -0.5)
            key_pos = lax.broadcasted_iota(jnp.int32, (block, keys), 1)
            q_pos = blk * block + lax.broadcasted_iota(jnp.int32, (block, keys), 0)
            scores = jnp.where((key_pos <= q_pos) & (key_pos < seq_len), scores, -1e30)
            top = jnp.max(scores, axis=-1, keepdims=True)
            weights = jnp.exp(scores - top)
            probs = (weights / jnp.sum(weights, axis=-1, keepdims=True)).astype(BF16)
            out_ref[...] = jnp.dot(probs, v_ref[:keys, :], preferred_element_type=F32).astype(BF16)


def attend(qkv, lens, n_heads, head_dim, block=512):
    n_seq, length, _ = qkv.shape
    n_blocks = length // block
    flops = 4 * n_seq * n_heads * length * length * head_dim * 5 // 8
    return pl.pallas_call(
        functools.partial(attend_kernel, block, n_blocks),
        grid_spec=pltpu.PrefetchScalarGridSpec(
            num_scalar_prefetch=1,
            grid=(n_seq, n_heads, n_blocks),
            in_specs=[
                pl.BlockSpec((None, block, head_dim), lambda c, i, b, s: (c, b, i)),
                pl.BlockSpec((None, length, head_dim), lambda c, i, b, s: (c, 0, n_heads)),
                pl.BlockSpec((None, length, head_dim), lambda c, i, b, s: (c, 0, n_heads + 1)),
            ],
            out_specs=pl.BlockSpec((None, block, head_dim), lambda c, i, b, s: (c, b, i)),
        ),
        out_shape=jax.ShapeDtypeStruct((n_seq, length, n_heads * head_dim), BF16),
        compiler_params=pltpu.CompilerParams(vmem_limit_bytes=VMEM_LIMIT),
        cost_estimate=pl.CostEstimate(flops=flops, bytes_accessed=4 * n_seq * n_heads * length * head_dim * 4, transcendentals=n_seq * n_heads * length * length),
        name="attend",
    )(lens, qkv, qkv, qkv)


def same_kernel(x_ref, out_ref):
    out_ref[...] = x_ref[...]


def same(x):
    return pl.pallas_call(same_kernel, out_shape=jax.ShapeDtypeStruct(x.shape, x.dtype), name="same")(x)


def solution(mesh):
    batch_axes = ("rep", "data")
    n_model = mesh.shape["model"]
    swap = [(0, 1), (1, 0)]

    def across(value):
        return lax.ppermute(value, "data", swap)

    def gather_seq(value):
        return lax.all_gather(value, "model", axis=1, tiled=True)

    def scatter_seq(value):
        return lax.psum_scatter(value, "model", scatter_dimension=1, tiled=True)

    def local_body(x_loc, lens_loc, gamma_loc, w_in_loc, w_kv_loc, w_out_loc):
        n_batch, seq_loc, d_model = x_loc.shape
        half = d_model // 2
        head_dim = w_kv_loc.shape[2] // 2
        out_local = w_out_loc.shape[1]
        ff = w_in_loc.shape[2] - out_local
        attn_cols = out_local - ff
        n_heads = attn_cols // head_dim
        seq = seq_loc * n_model
        rows = n_batch * seq
        mine = lax.axis_index("data")
        theirs = 1 - mine
        slot = lax.axis_index("model")

        def swap_halves(value):
            return jnp.concatenate([value[..., half:], value[..., :half]], axis=-1)

        def own_first(value):
            return jnp.where(mine == 0, value, swap_halves(value))

        def cols(layer, start, width):
            return lax.dynamic_slice(w_in_loc, (layer, 0, start), (1, half, width))[0]

        gamma = jnp.concatenate([gamma_loc, across(gamma_loc)], axis=-1)
        lens_all = jnp.concatenate([lens_loc, across(lens_loc)])
        part = half // n_model
        kv_part = across(lax.dynamic_slice(w_kv_loc, (0, slot * part, 0), (2, part, 2 * head_dim)))
        kv_oth = gather_seq(kv_part)
        w_kv = jnp.concatenate([w_kv_loc, kv_oth], axis=1)

        b_q, b_ff = attn_cols // 2, ff // 2
        b_chunk = 512
        hidden = own_first(x_loc)
        normed = rms_norm(hidden, gamma[0])
        q_oth = across(cols(0, theirs * b_q, b_q))
        normed_oth = across(swap_halves(normed))
        in_oth = []
        for c in range(b_ff // b_chunk):
            start = attn_cols + theirs * b_ff + c * b_chunk
            in_oth.append(across(jnp.concatenate([cols(0, start, b_chunk), cols(0, ff + start, b_chunk)], axis=1)))

        def out_rows(which):
            top = lax.dynamic_slice(w_out_loc, (0, which * b_q, 0), (1, b_q, half))[0]
            low = lax.dynamic_slice(w_out_loc, (0, attn_cols + which * b_ff, 0), (1, b_ff, half))[0]
            return jnp.concatenate([top, low], axis=0)

        out_oth = across(out_rows(theirs))

        a_chunk = 1024
        q1_oth = across(w_in_loc[1, :, :attn_cols])
        in1_oth = []
        for c in range(ff // a_chunk):
            start = attn_cols + c * a_chunk
            in1_oth.append(across(jnp.concatenate([w_in_loc[1, :, start:start + a_chunk], w_in_loc[1, :, ff + start:ff + start + a_chunk]], axis=1)))
        o_chunk = 256
        out1_oth = [across(w_out_loc[1, :, c:c + o_chunk]) for c in range(0, half, o_chunk)]

        shift = (mine * (b_ff // 512)).astype(jnp.int32).reshape(1)
        none = jnp.zeros((1,), jnp.int32)

        w_qkv = jnp.concatenate([jnp.concatenate([cols(0, mine * b_q, b_q), q_oth], axis=0), w_kv[0]], axis=1)
        w_out0 = jnp.concatenate([out_rows(mine), out_oth], axis=1)
        groups = []
        for group, tokens in enumerate((normed, normed_oth)):
            h_full = gather_seq(tokens).reshape(rows, d_model)
            qkv = jnp.dot(h_full, w_qkv, preferred_element_type=F32).astype(BF16).reshape(n_batch, seq, -1)
            attn = attend(qkv, lens_all[group * n_batch:(group + 1) * n_batch], n_heads // 2, head_dim)
            lhs = [attn.reshape(rows, -1)]
            for c in range(b_ff // b_chunk):
                lhs.append(gated(h_full, w_in_loc, in_oth[c], 0, shift, attn_cols + c * b_chunk, attn_cols + ff + c * b_chunk, b_chunk))
            groups.append(lhs)
        z_parts = []
        for lhs in groups:
            z = project(lhs, w_out0).reshape(n_batch, seq, d_model)
            z_parts.append(scatter_seq(z))
        z_got = across(swap_halves(z_parts[1]))
        hidden = (hidden.astype(F32) + (z_parts[0].astype(F32) + z_got.astype(F32))).astype(BF16)

        gain1 = same(gamma[1:2])[0]
        normed = rms_norm(hidden, gain1)
        h_full = gather_seq(normed).reshape(rows, d_model)
        w_qkv = jnp.concatenate([jnp.concatenate([w_in_loc[1, :, :attn_cols], q1_oth], axis=0), w_kv[1]], axis=1)
        qkv = jnp.dot(h_full, w_qkv, preferred_element_type=F32).astype(BF16).reshape(n_batch, seq, -1)
        attn = attend(qkv, lens_loc, n_heads, head_dim)
        lhs = [attn.reshape(rows, -1)]
        for c in range(ff // a_chunk):
            lhs.append(gated(h_full, w_in_loc, in1_oth[c], 1, none, attn_cols + c * a_chunk, attn_cols + ff + c * a_chunk, a_chunk))
        z_all = [scatter_seq(project(lhs, w_out_loc, layer=1).reshape(n_batch, seq, half))]
        for piece in out1_oth:
            z_all.append(scatter_seq(project(lhs, piece).reshape(n_batch, seq, o_chunk)))
        z = jnp.concatenate(z_all, axis=-1)
        hidden = (hidden.astype(F32) + z.astype(F32)).astype(BF16)
        return own_first(hidden)

    in_specs = (
        P(batch_axes, "model", None),
        P(batch_axes),
        P(None, "data"),
        P(None, "data", "model"),
        P(None, "data", None),
        P(None, "model", "data"),
    )
    return jax.shard_map(local_body, mesh=mesh, in_specs=in_specs, out_specs=P(batch_axes, "model", None), check_vma=False)
```

time: 2330 us -> 1640 us (0.70)
  Pallas kernels: 0 us -> 645 us
  matrix products: 697 us -> 61.4 us
  waiting for transfers between devices: 1220 us -> 754 us
  other arithmetic: 206 us -> 63.9 us
  local copies, waits for them, and re-layouts: 158 us -> 72.1 us
    all_gather x8 -> x4, waiting for transfers between devices: 984 us -> 0.57 us  [gather_seq(): return lax.all_gather(value, 'model', axis=1, tiled=True)]
    pallas_call x0 -> x23, Pallas kernels: none -> 645 us  [the longest x12 349 us: gated(): pl.pallas_call(gated_kernel, grid_spec=pltpu.PrefetchScalarGridSpec(num_s...]
    dot_general x24 -> x3, matrix products: 697 us -> 61.4 us  [local_body(): jnp.dot(h_full, w_qkv, preferred_element_type=F32).astype(BF16)]
    ppermute x0 -> x20, waiting for transfers between devices: none -> 620 us  [across(): return lax.ppermute(value, 'data', swap)]
    sub x8 -> x0, other arithmetic: 163 us -> none  [one_block(): attn_probs = jax.nn.softmax(scores, axis=-1).astype(jnp.bfloat16)]
    reduce_scatter x2 -> x7, waiting for transfers between devices: 233 us -> 132 us  [scatter_seq(): return lax.psum_scatter(value, 'model', scatter_dimension=1, tiled=True)]
    slice x8 -> x4, local copies, waits for them, and re-layouts: 57.2 us -> 10.2 us  [swap_halves(): return jnp.concatenate([value[..., half:], value[..., :half]], axis=-1)]
    transpose x2 -> x0, local copies, waits for them, and re-layouts: 46 us -> none  [local_step(): jnp.einsum('nbqe,ed->bnqd', attn_blocks, w_out_full[:attn_cols], preferre...]
  transfers between devices with their start and end apart: 10 -> 31, of which waited for: 6 -> 17; matrix products, arithmetic and copies ran while one was open for 34% -> 10% of each run, Pallas kernels for 0% -> 34%
where the time goes in v1:
time: 1640 us; the launch traced here: 1630 us
  waiting for transfers between devices  754 us (46%)
  Pallas kernels  645 us (39%)
  local copies, waits for them, and re-layouts  72.1 us (4%)
  other arithmetic  63.9 us (4%)
  matrix products  61.4 us (4%)
  starting transfers between devices  22.9 us (1%)
    ppermute x20, waiting for transfers between devices, across(): return lax.ppermute(value, 'data', swap)  620 us
    pallas_call x12, Pallas kernels, gated(): pl.pallas_call(gated_kernel, grid_spec=pltpu.PrefetchScalarGridSpec(num_s...  349 us
    pallas_call x7, Pallas kernels, project(): pl.pallas_call(functools.partial(project_kernel, len(lhs)), grid=(cols //...  220 us
    reduce_scatter x7, waiting for transfers between devices, scatter_seq(): return lax.psum_scatter(value, 'model', scatter_dimension=1, tiled=True)  132 us
    pallas_call x3, Pallas kernels, attend(): pl.pallas_call(functools.partial(attend_kernel, block, n_blocks), grid_sp...  74.7 us
    dot_general x3, matrix products, local_body(): jnp.dot(h_full, w_qkv, preferred_element_type=F32).astype(BF16)  61.4 us
  transfers between devices with their start and end apart: 31, of which 17 were waited for; matrix products, arithmetic and copies ran while one was open for 10% of the time, Pallas kernels for 34%

profile of v1, /device:TPU:0, one launch (start us, length us, event | category | flops | bytes accessed | tf_op | source)
XLA Modules:
  0.0 1632.6 jit_solution(3898979474620943097)
XLA Ops:
  31.3 100.4 %collective-permute-done.2 = bf16[2,256,512]{2,1,0:T(8,128)(2,1)S(1)} collective-permute-done((bf16[2,256,512]{2,1,0:T(8,128)(2,1)S(1)}, bf16[2,256,512]{2,1,0:T(8,128)(2,1)S(1)}, u32[]{:S(2)}, u32[]{:S(2)}) %collective-permute-start.2) | collective-permute-done | bytes 524320 | tf_op jit(solution)/shard_map/ppermute | solution.py:145
  176.3 74.3 %collective-permute-done.7 = bf16[2304,1024]{1,0:T(8,128)(2,1)} collective-permute-done((bf16[2304,1024]{1,0:T(8,128)(2,1)}, bf16[2304,1024]{1,0:T(8,128)(2,1)}, u32[]{:S(2)}, u32[]{:S(2)}) %collective-permute-start.7) | collective-permute-done | bytes 4718624 | tf_op jit(solution)/shard_map/ppermute | solution.py:145
  265.4 41.2 %collective-permute-done.3.g_oth.u_oth = bf16[1024,1024]{1,0:T(8,128)(2,1)S(1)} collective-permute-done((bf16[1024,1024]{1,0:T(8,128)(2,1)}, bf16[1024,1024]{1,0:T(8,128)(2,1)S(1)}, u32[]{:S(2)}, u32[]{:S(2)}) %collective-permute-start.3) | collective-permute-done | bytes 2097184 | tf_op jit(solution)/shard_map/ppermute | solution.py:145
  308.0 22.9 %gated.16.refs_1_ = bf16[4096,512]{1,0:T(8,128)(2,1)} custom-call(s32[1]{0:T(128)} %bitcast.7.idx_ref, bf16[4096,2048]{1,0:T(8,128)(2,1)} %bitcast.85, bf16[2,1024,8704]{2,1,0:T(8,128)(2,1)} %u_own.23, bf16[2,1024,8704]{2,1,0:T(8,128)(2,1)} %u_own.23, bf16[1024,1024]{1,0:T(8,128)(2,1)} %copy-done.2, bf16[1024,1024]{1,0:T(8,128)(2,1)} %copy-done.2), custom_call_target="tpu_custom_call" | custom-call | flops 17179869184 | bytes 25165824 | tf_op jit(solution)/shard_map/gated/pallas_call | solution.py:38
  351.7 22.9 %gated.17.refs_2_ = bf16[4096,512]{1,0:T(8,128)(2,1)} custom-call(s32[1]{0:T(128)} %bitcast.7.idx_ref, bf16[4096,2048]{1,0:T(8,128)(2,1)} %bitcast.87, bf16[2,1024,8704]{2,1,0:T(8,128)(2,1)} %u_own.23, bf16[2,1024,8704]{2,1,0:T(8,128)(2,1)} %u_own.23, bf16[1024,1024]{1,0:T(8,128)(2,1)} %collective-permute-done.4.g_oth.u_oth, ...), custom_call_target="tpu_custom_call" | custom-call | flops 17179869184 | bytes 25165824 | tf_op jit(solution)/shard_map/gated/pallas_call | solution.py:38
  439.5 22.9 %gated.19.refs_4_ = bf16[4096,512]{1,0:T(8,128)(2,1)} custom-call(s32[1]{0:T(128)} %bitcast.7.idx_ref, bf16[4096,2048]{1,0:T(8,128)(2,1)} %bitcast.89, bf16[2,1024,8704]{2,1,0:T(8,128)(2,1)} %u_own.23, bf16[2,1024,8704]{2,1,0:T(8,128)(2,1)} %u_own.23, bf16[1024,1024]{1,0:T(8,128)(2,1)} %collective-permute-done.6.g_oth.u_oth, ...), custom_call_target="tpu_custom_call" | custom-call | flops 17179869184 | bytes 25165824 | tf_op jit(solution)/shard_map/gated/pallas_call | solution.py:38
  462.4 48.9 %project.8 = bf16[4096,2048]{1,0:T(8,128)(2,1)} custom-call(bf16[4096,256]{1,0:T(8,128)(2,1)} %bitcast.108, bf16[4096,512]{1,0:T(8,128)(2,1)} %gated.16.refs_1_, bf16[4096,512]{1,0:T(8,128)(2,1)} %gated.17.refs_2_, bf16[4096,512]{1,0:T(8,128)(2,1)} %gated.18.refs_3_, bf16[4096,512]{1,0:T(8,128)(2,1)} %gated.19.refs_4_, ...), custom_call_target="tpu_custom_call" | custom-call | flops 38654705664 | bytes 101711872 | tf_op jit(solution)/shard_map/project/pallas_call | solution.py:78
  552.3 22.9 %gated.12.refs_1_ = bf16[4096,512]{1,0:T(8,128)(2,1)} custom-call(s32[1]{0:T(128)} %bitcast.7.idx_ref, bf16[4096,2048]{1,0:T(8,128)(2,1)} %bitcast.81, bf16[2,1024,8704]{2,1,0:T(8,128)(2,1)} %u_own.23, bf16[2,1024,8704]{2,1,0:T(8,128)(2,1)} %u_own.23, bf16[1024,1024]{1,0:T(8,128)(2,1)} %copy-done.2, bf16[1024,1024]{1,0:T(8,128)(2,1)} %copy-done.2), custom_call_target="tpu_custom_call" | custom-call | flops 17179869184 | bytes 25165824 | tf_op jit(solution)/shard_map/gated/pallas_call | solution.py:38
  598.0 22.9 %gated.14.refs_3_ = bf16[4096,512]{1,0:T(8,128)(2,1)} custom-call(s32[1]{0:T(128)} %bitcast.7.idx_ref, bf16[4096,2048]{1,0:T(8,128)(2,1)} %bitcast.83, bf16[2,1024,8704]{2,1,0:T(8,128)(2,1)} %u_own.23, bf16[2,1024,8704]{2,1,0:T(8,128)(2,1)} %u_own.23, bf16[1024,1024]{1,0:T(8,128)(2,1)} %collective-permute-done.5.g_oth.u_oth, ...), custom_call_target="tpu_custom_call" | custom-call | flops 17179869184 | bytes 25165824 | tf_op jit(solution)/shard_map/gated/pallas_call | solution.py:38
  643.6 48.9 %project.7 = bf16[4096,2048]{1,0:T(8,128)(2,1)} custom-call(bf16[4096,256]{1,0:T(8,128)(2,1)} %bitcast.109, bf16[4096,512]{1,0:T(8,128)(2,1)} %gated.12.refs_1_, bf16[4096,512]{1,0:T(8,128)(2,1)} %gated.13.refs_2_, bf16[4096,512]{1,0:T(8,128)(2,1)} %gated.14.refs_3_, bf16[4096,512]{1,0:T(8,128)(2,1)} %gated.15.refs_4_, ...), custom_call_target="tpu_custom_call" | custom-call | flops 38654705664 | bytes 101711872 | tf_op jit(solution)/shard_map/project/pallas_call | solution.py:78
  700.2 111.4 %reduce-scatter.8.cloned.1.call-done = bf16[2,512,2048]{2,1,0:T(8,128)(2,1)} async-done(((bf16[2,2048,2048]{2,1,0:T(8,128)(2,1)}), bf16[2,512,2048]{2,1,0:T(8,128)(2,1)}) %reduce-scatter.8.cloned.1.call-update) | async-done | bytes 4194320 | tf_op jit(solution)/shard_map/reduce_scatter | solution.py:151
  844.8 80.6 %collective-permute-done.12.g_oth.u_oth = bf16[1024,2048]{1,0:T(8,128)(2,1)} collective-permute-done((bf16[1024,2048]{1,0:T(8,128)(2,1)S(1)}, bf16[1024,2048]{1,0:T(8,128)(2,1)}, u32[]{:S(2)}, u32[]{:S(2)}) %collective-permute-start.12) | collective-permute-done | bytes 4194336 | tf_op jit(solution)/shard_map/ppermute | solution.py:145
  926.0 41.5 %gated.20.refs_1_ = bf16[4096,1024]{1,0:T(8,128)(2,1)} custom-call(s32[1]{0:T(128)} %constant.70.clone.1.idx_ref, bf16[4096,2048]{1,0:T(8,128)(2,1)} %bitcast.112, bf16[2,1024,8704]{2,1,0:T(8,128)(2,1)} %u_own.23, bf16[2,1024,8704]{2,1,0:T(8,128)(2,1)} %u_own.23, bf16[1024,2048]{1,0:T(8,128)(2,1)} %collective-permute-done.12.g_oth.u_oth, ...), custom_call_target="tpu_custom_call" | custom-call | flops 34359738368 | bytes 50331648 | tf_op jit(solution)/shard_map/gated/pallas_call | solution.py:38
  990.0 47.7 %collective-permute-done.13.g_oth.u_oth = bf16[1024,2048]{1,0:T(8,128)(2,1)} collective-permute-done((bf16[1024,2048]{1,0:T(8,128)(2,1)}, bf16[1024,2048]{1,0:T(8,128)(2,1)}, u32[]{:S(2)}, u32[]{:S(2)}) %collective-permute-start.13) | collective-permute-done | bytes 4194336 | tf_op jit(solution)/shard_map/ppermute | solution.py:145
  1037.8 41.9 %gated.21.refs_2_ = bf16[4096,1024]{1,0:T(8,128)(2,1)} custom-call(s32[1]{0:T(128)} %constant.70.clone.1.idx_ref, bf16[4096,2048]{1,0:T(8,128)(2,1)} %bitcast.114, bf16[2,1024,8704]{2,1,0:T(8,128)(2,1)} %u_own.23, bf16[2,1024,8704]{2,1,0:T(8,128)(2,1)} %u_own.23, bf16[1024,2048]{1,0:T(8,128)(2,1)} %collective-permute-done.13.g_oth.u_oth, ...), custom_call_target="tpu_custom_call" | custom-call | flops 34359738368 | bytes 50331648 | tf_op jit(solution)/shard_map/gated/pallas_call | solution.py:38
  1079.7 35.7 %attend.5 = bf16[2,2048,512]{2,1,0:T(8,128)(2,1)} custom-call(s32[2]{0:T(128)} %lens_ref.3, bf16[2,2048,1024]{2,1,0:T(8,128)(2,1)} %bitcast.117, bf16[2,2048,1024]{2,1,0:T(8,128)(2,1)} %bitcast.118, bf16[2,2048,1024]{2,1,0:T(8,128)(2,1)} %bitcast.119), custom_call_target="tpu_custom_call" | custom-call | flops 10737418240 | bytes 33554432 | tf_op jit(solution)/shard_map/attend/pallas_call | solution.py:112
  1127.6 41.4 %gated.22.refs_3_ = bf16[4096,1024]{1,0:T(8,128)(2,1)} custom-call(s32[1]{0:T(128)} %constant.70.clone.1.idx_ref, bf16[4096,2048]{1,0:T(8,128)(2,1)} %bitcast.115, bf16[2,1024,8704]{2,1,0:T(8,128)(2,1)} %u_own.23, bf16[2,1024,8704]{2,1,0:T(8,128)(2,1)} %u_own.23, bf16[1024,2048]{1,0:T(8,128)(2,1)} %collective-permute-done.14.g_oth.u_oth, ...), custom_call_target="tpu_custom_call" | custom-call | flops 34359738368 | bytes 50331648 | tf_op jit(solution)/shard_map/gated/pallas_call | solution.py:38
  1169.0 46.7 %collective-permute-done.15.g_oth.u_oth = bf16[1024,2048]{1,0:T(8,128)(2,1)} collective-permute-done((bf16[1024,2048]{1,0:T(8,128)(2,1)}, bf16[1024,2048]{1,0:T(8,128)(2,1)}, u32[]{:S(2)}, u32[]{:S(2)}) %collective-permute-start.15) | collective-permute-done | bytes 4194336 | tf_op jit(solution)/shard_map/ppermute | solution.py:145
  1215.8 41.5 %gated.23.refs_4_ = bf16[4096,1024]{1,0:T(8,128)(2,1)} custom-call(s32[1]{0:T(128)} %constant.70.clone.1.idx_ref, bf16[4096,2048]{1,0:T(8,128)(2,1)} %bitcast.116, bf16[2,1024,8704]{2,1,0:T(8,128)(2,1)} %u_own.23, bf16[2,1024,8704]{2,1,0:T(8,128)(2,1)} %u_own.23, bf16[1024,2048]{1,0:T(8,128)(2,1)} %collective-permute-done.15.g_oth.u_oth, ...), custom_call_target="tpu_custom_call" | custom-call | flops 34359738368 | bytes 50331648 | tf_op jit(solution)/shard_map/gated/pallas_call | solution.py:38
  1257.3 47.1 %project.9 = bf16[4096,1024]{1,0:T(8,128)(2,1)} custom-call(bf16[4096,512]{1,0:T(8,128)(2,1)} %bitcast.90, bf16[4096,1024]{1,0:T(8,128)(2,1)} %gated.20.refs_1_, bf16[4096,1024]{1,0:T(8,128)(2,1)} %gated.21.refs_2_, bf16[4096,1024]{1,0:T(8,128)(2,1)} %gated.22.refs_3_, bf16[4096,1024]{1,0:T(8,128)(2,1)} %gated.23.refs_4_, bf16[2,4608,1024]{2,1,0:T(8,128)(2,1)} %refs_5_.1), custom_call_target="tpu_custom_call" | custom-call | flops 38654705664 | bytes 93323264 | tf_op jit(solution)/shard_map/project/pallas_call | solution.py:78
  1312.7 49.5 %collective-permute-done.16.refs_5_ = bf16[4608,256]{1,0:T(8,128)(2,1)} collective-permute-done((bf16[4608,256]{1,0:T(8,128)(2,1)S(1)}, bf16[4608,256]{1,0:T(8,128)(2,1)}, u32[]{:S(2)}, u32[]{:S(2)}) %collective-permute-start.16) | collective-permute-done | bytes 2359328 | tf_op jit(solution)/shard_map/ppermute | solution.py:145
  1382.5 48.7 %collective-permute-done.17.refs_5_ = bf16[4608,256]{1,0:T(8,128)(2,1)} collective-permute-done((bf16[4608,256]{1,0:T(8,128)(2,1)}, bf16[4608,256]{1,0:T(8,128)(2,1)}, u32[]{:S(2)}, u32[]{:S(2)}) %collective-permute-start.17) | collective-permute-done | bytes 2359328 | tf_op jit(solution)/shard_map/ppermute | solution.py:145
  1451.8 47.8 %collective-permute-done.18.refs_5_ = bf16[4608,256]{1,0:T(8,128)(2,1)} collective-permute-done((bf16[4608,256]{1,0:T(8,128)(2,1)}, bf16[4608,256]{1,0:T(8,128)(2,1)}, u32[]{:S(2)}, u32[]{:S(2)}) %collective-permute-start.18) | collective-permute-done | bytes 2359328 | tf_op jit(solution)/shard_map/ppermute | solution.py:145
  1520.1 46.7 %collective-permute-done.19.refs_5_ = bf16[4608,256]{1,0:T(8,128)(2,1)} collective-permute-done((bf16[4608,256]{1,0:T(8,128)(2,1)S(1)}, bf16[4608,256]{1,0:T(8,128)(2,1)}, u32[]{:S(2)}, u32[]{:S(2)}) %collective-permute-start.19) | collective-permute-done | bytes 2359328 | tf_op jit(solution)/shard_map/ppermute | solution.py:145
  (148 shorter events, 462.3 us)
Async XLA Ops:
  6.5 161.8 %all-gather.7.cloned.1.call-start = ((), (), s32[]{:S(2)}) async-start(), calls=%async_computation.8 | async-start | bytes 2621440 | tf_op jit(solution)/shard_map/all_gather | solution.py:148
  28.1 104.4 %collective-permute-start.9 = (bf16[2,512,2048]{2,1,0:T(8,128)(2,1)}, bf16[2,512,2048]{2,1,0:T(8,128)(2,1)}, u32[]{:S(2)}, u32[]{:S(2)}) collective-permute-start(bf16[2,512,2048]{2,1,0:T(8,128)(2,1)} %pad_maximum_fusion.2), channel_id=1, source_target_pairs={{0,4},{4,0},{1,5},{5,1},{2,6},{6,2},{3,7},{7,3}} | collective-permute-start | bytes 12582920 | tf_op jit(solution)/shard_map/ppermute | solution.py:145
  29.2 102.4 %collective-permute-start.2 = (bf16[2,256,512]{2,1,0:T(8,128)(2,1)S(1)}, bf16[2,256,512]{2,1,0:T(8,128)(2,1)S(1)}, u32[]{:S(2)}, u32[]{:S(2)}) collective-permute-start(bf16[2,256,512]{2,1,0:T(8,128)(2,1)S(1)} %constant_dynamic-slice_fusion), channel_id=1, source_target_pairs={{0,4},{4,0},{1,5},{5,1},{2,6},{6,2},{3,7},{7,3}} | collective-permute-start | bytes 1572872 | tf_op jit(solution)/shard_map/ppermute | solution.py:145
  132.4 174.7 %all-gather.9.cloned.1.call-start = ((), (), s32[]{:S(2)}) async-start(), calls=%async_computation.10 | async-start | bytes 20971520 | tf_op jit(solution)/shard_map/all_gather | solution.py:148
  133.2 378.2 %all-gather.5.cloned.1.call-start = ((), (), s32[]{:S(2)}) async-start(), calls=%async_computation.7 | async-start | bytes 20971520 | tf_op jit(solution)/shard_map/all_gather | solution.py:148
  133.9 558.6 %reduce-scatter.10.cloned.1.call-start = ((), (), s32[]{:S(2)}) async-start(), calls=%async_computation.11 | async-start | bytes 20971520 | tf_op jit(solution)/shard_map/reduce_scatter | solution.py:151
  145.6 105.0 %collective-permute-start.7 = (bf16[2304,1024]{1,0:T(8,128)(2,1)}, bf16[2304,1024]{1,0:T(8,128)(2,1)}, u32[]{:S(2)}, u32[]{:S(2)}) collective-permute-start(bf16[2304,1024]{1,0:T(8,128)(2,1)} %pad_maximum_fusion.1), channel_id=1, source_target_pairs={{0,4},{4,0},{1,5},{5,1},{2,6},{6,2},{3,7},{7,3}} | collective-permute-start | bytes 14155784 | tf_op jit(solution)/shard_map/ppermute | solution.py:145
  146.1 228.5 %collective-permute-start.8 = (s32[2]{0:T(128)S(1)}, s32[2]{0:T(128)S(1)}, u32[]{:S(2)}, u32[]{:S(2)}) collective-permute-start(s32[2]{0:T(128)S(1)} %copy-done.13), channel_id=1, source_target_pairs={{0,4},{4,0},{1,5},{5,1},{2,6},{6,2},{3,7},{7,3}} | collective-permute-start | bytes 32 | tf_op jit(solution)/shard_map/ppermute | solution.py:145
  149.9 181.0 %collective-permute-start.1 = (bf16[1024,256]{1,0:T(8,128)(2,1)}, bf16[1024,256]{1,0:T(8,128)(2,1)}, u32[]{:S(2)}, u32[]{:S(2)}) collective-permute-start(bf16[1024,256]{1,0:T(8,128)(2,1)} %get-tuple-element.27), channel_id=1, source_target_pairs={{0,4},{4,0},{1,5},{5,1},{2,6},{6,2},{3,7},{7,3}} | collective-permute-start | bytes 1572872 | tf_op jit(solution)/shard_map/ppermute | solution.py:145
  158.1 148.6 %collective-permute-start.3 = (bf16[1024,1024]{1,0:T(8,128)(2,1)}, bf16[1024,1024]{1,0:T(8,128)(2,1)S(1)}, u32[]{:S(2)}, u32[]{:S(2)}) collective-permute-start(bf16[1024,1024]{1,0:T(8,128)(2,1)} %pad_maximum_fusion.9), channel_id=1, source_target_pairs={{0,4},{4,0},{1,5},{5,1},{2,6},{6,2},{3,7},{7,3}} | collective-permute-start | bytes 6291464 | tf_op jit(solution)/shard_map/ppermute | solution.py:145
  161.2 190.5 %collective-permute-start.4 = (bf16[1024,1024]{1,0:T(8,128)(2,1)}, bf16[1024,1024]{1,0:T(8,128)(2,1)}, u32[]{:S(2)}, u32[]{:S(2)}) collective-permute-start(bf16[1024,1024]{1,0:T(8,128)(2,1)} %pad_maximum_fusion.10), channel_id=1, source_target_pairs={{0,4},{4,0},{1,5},{5,1},{2,6},{6,2},{3,7},{7,3}} | collective-permute-start | bytes 6291464 | tf_op jit(solution)/shard_map/ppermute | solution.py:145
  250.6 146.1 %collective-permute-start.5 = (bf16[1024,1024]{1,0:T(8,128)(2,1)}, bf16[1024,1024]{1,0:T(8,128)(2,1)}, u32[]{:S(2)}, u32[]{:S(2)}) collective-permute-start(bf16[1024,1024]{1,0:T(8,128)(2,1)} %pad_maximum_fusion.11), channel_id=1, source_target_pairs={{0,4},{4,0},{1,5},{5,1},{2,6},{6,2},{3,7},{7,3}} | collective-permute-start | bytes 6291464 | tf_op jit(solution)/shard_map/ppermute | solution.py:145
  306.7 132.8 %collective-permute-start.6 = (bf16[1024,1024]{1,0:T(8,128)(2,1)}, bf16[1024,1024]{1,0:T(8,128)(2,1)}, u32[]{:S(2)}, u32[]{:S(2)}) collective-permute-start(bf16[1024,1024]{1,0:T(8,128)(2,1)} %pad_maximum_fusion.12), channel_id=1, source_target_pairs={{0,4},{4,0},{1,5},{5,1},{2,6},{6,2},{3,7},{7,3}} | collective-permute-start | bytes 6291464 | tf_op jit(solution)/shard_map/ppermute | solution.py:145
  511.3 300.4 %reduce-scatter.8.cloned.1.call-start = ((), (), s32[]{:S(2)}) async-start(), calls=%async_computation.9 | async-start | bytes 20971520 | tf_op jit(solution)/shard_map/reduce_scatter | solution.py:151
  692.5 233.5 %all-gather.11.cloned.1.call-start = ((), (), s32[]{:S(2)}) async-start(), calls=%async_computation.12 | async-start | bytes 20971520 | tf_op jit(solution)/shard_map/all_gather | solution.py:148
  698.0 113.6 %collective-permute-start.10 = (bf16[2,512,2048]{2,1,0:T(8,128)(2,1)}, bf16[2,512,2048]{2,1,0:T(8,128)(2,1)}, u32[]{:S(2)}, u32[]{:S(2)}) collective-permute-start(bf16[2,512,2048]{2,1,0:T(8,128)(2,1)} %pad_maximum_fusion.3), channel_id=1, source_target_pairs={{0,4},{4,0},{1,5},{5,1},{2,6},{6,2},{3,7},{7,3}} | collective-permute-start | bytes 12582920 | tf_op jit(solution)/shard_map/ppermute | solution.py:145
  822.7 763.2 %reduce-scatter.12.cloned.1.call-start = ((), (), s32[]{:S(2)}) async-start(), calls=%async_computation.13 | async-start | bytes 10485760 | tf_op jit(solution)/shard_map/reduce_scatter | solution.py:151
  833.1 134.4 %collective-permute-start.11 = (bf16[1024,512]{1,0:T(8,128)(2,1)S(1)}, bf16[1024,512]{1,0:T(8,128)(2,1)}, u32[]{:S(2)}, u32[]{:S(2)}) collective-permute-start(bf16[1024,512]{1,0:T(8,128)(2,1)S(1)} %copy-done.9), channel_id=1, source_target_pairs={{0,4},{4,0},{1,5},{5,1},{2,6},{6,2},{3,7},{7,3}} | collective-permute-start | bytes 3145736 | tf_op jit(solution)/shard_map/ppermute | solution.py:145
  836.9 200.9 %collective-permute-start.13 = (bf16[1024,2048]{1,0:T(8,128)(2,1)}, bf16[1024,2048]{1,0:T(8,128)(2,1)}, u32[]{:S(2)}, u32[]{:S(2)}) collective-permute-start(bf16[1024,2048]{1,0:T(8,128)(2,1)} %pad_maximum_fusion.5), channel_id=1, source_target_pairs={{0,4},{4,0},{1,5},{5,1},{2,6},{6,2},{3,7},{7,3}} | collective-permute-start | bytes 12582920 | tf_op jit(solution)/shard_map/ppermute | solution.py:145
  840.5 287.1 %collective-permute-start.14 = (bf16[1024,2048]{1,0:T(8,128)(2,1)}, bf16[1024,2048]{1,0:T(8,128)(2,1)}, u32[]{:S(2)}, u32[]{:S(2)}) collective-permute-start(bf16[1024,2048]{1,0:T(8,128)(2,1)} %pad_maximum_fusion.6), channel_id=1, source_target_pairs={{0,4},{4,0},{1,5},{5,1},{2,6},{6,2},{3,7},{7,3}} | collective-permute-start | bytes 12582920 | tf_op jit(solution)/shard_map/ppermute | solution.py:145
  843.5 372.2 %collective-permute-start.15 = (bf16[1024,2048]{1,0:T(8,128)(2,1)}, bf16[1024,2048]{1,0:T(8,128)(2,1)}, u32[]{:S(2)}, u32[]{:S(2)}) collective-permute-start(bf16[1024,2048]{1,0:T(8,128)(2,1)} %pad_maximum_fusion.7), channel_id=1, source_target_pairs={{0,4},{4,0},{1,5},{5,1},{2,6},{6,2},{3,7},{7,3}} | collective-permute-start | bytes 12582920 | tf_op jit(solution)/shard_map/ppermute | solution.py:145
  1304.4 284.6 %reduce-scatter.14.cloned.1.call-start = ((), (), s32[]{:S(2)}) async-start(), calls=%async_computation.14 | async-start | bytes 2621440 | tf_op jit(solution)/shard_map/reduce_scatter | solution.py:151
  1381.0 210.0 %reduce-scatter.16.cloned.1.call-start = ((), (), s32[]{:S(2)}) async-start(), calls=%async_computation.15 | async-start | bytes 2621440 | tf_op jit(solution)/shard_map/reduce_scatter | solution.py:151
  1450.0 143.0 %reduce-scatter.18.cloned.1.call-start = ((), (), s32[]{:S(2)}) async-start(), calls=%async_computation.16 | async-start | bytes 2621440 | tf_op jit(solution)/shard_map/reduce_scatter | solution.py:151
  (22 other events, 649.6 us)
Sparse Core Ops, SparseCore 0:
  132.6 19.7 all-gather.6
  153.9 103.1 all-gather.8
  258.6 103.1 all-gather.4
  511.4 119.3 reduce-scatter.9
  692.6 119.0 reduce-scatter.7
  822.8 103.1 all-gather.10
  1304.5 65.7 reduce-scatter.11
  1381.1 25.6 reduce-scatter.13
  1450.1 26.3 reduce-scatter.15
  1518.4 27.6 reduce-scatter.17
  1586.0 29.0 reduce-scatter.19

commit v2 on v0

v2 whole, which is shorter than its diff:
```python
import functools

import jax
import jax.numpy as jnp
from jax import lax
from jax.experimental import pallas as pl
from jax.experimental.pallas import tpu as pltpu
from jax.sharding import PartitionSpec as P

EPSILON = 1e-6
PARAMS = pltpu.CompilerParams(vmem_limit_bytes=60 * 1024 * 1024)
BF16 = jnp.bfloat16
F32 = jnp.float32


def normalize(parts, gains):
    d_model = sum(p.shape[-1] for p in parts)
    square = sum(jnp.sum(p * p, axis=-1, keepdims=True) for p in parts)
    inv_rms = lax.rsqrt(square / d_model + EPSILON)
    return [(p * inv_rms * g.astype(F32)).astype(BF16) for p, g in zip(parts, gains)]


def first_norm_kernel(mine_ref, x_ref, gain_ref, hidden_ref, normed_ref):
    half = hidden_ref.shape[2]
    low, high = x_ref[:, :half], x_ref[:, half:]
    first = mine_ref[0] == 0
    parts = [jnp.where(first, low, high), jnp.where(first, high, low)]
    normed = normalize([p.astype(F32) for p in parts], [gain_ref[0:1, :], gain_ref[1:2, :]])
    for k in range(2):
        hidden_ref[k] = parts[k]
        normed_ref[k] = normed[k]


def first_norm(mine, x_loc, gain, which):
    _, seq_loc, d_model = x_loc.shape
    shape = (2, seq_loc, d_model // 2)
    whole = pl.BlockSpec(shape, lambda i, s: (0, 0, 0))
    return pl.pallas_call(
        first_norm_kernel,
        grid_spec=pltpu.PrefetchScalarGridSpec(
            num_scalar_prefetch=1,
            grid=(1,),
            in_specs=[pl.BlockSpec((None, seq_loc, d_model), lambda i, s: (which, 0, 0)), pl.BlockSpec(gain.shape, lambda i, s: (0, 0))],
            out_specs=[whole, whole],
        ),
        out_shape=[jax.ShapeDtypeStruct(shape, BF16)] * 2,
        compiler_params=PARAMS,
        cost_estimate=pl.CostEstimate(flops=3000000, bytes_accessed=6 * seq_loc * d_model, transcendentals=0),
        name="first_norm",
    )(mine, x_loc, gain)


def add_norm_kernel(hidden_ref, here_ref, there_ref, gain_ref, out_ref, normed_ref):
    parts = []
    for k in range(2):
        z = here_ref[k].astype(F32) + there_ref[1 - k].astype(F32)
        parts.append((hidden_ref[k].astype(F32) + z).astype(BF16))
        out_ref[k] = parts[k]
    normed = normalize([p.astype(F32) for p in parts], [gain_ref[0:1, :], gain_ref[1:2, :]])
    for k in range(2):
        normed_ref[k] = normed[k]


def add_norm(hidden, here, there, gain):
    return pl.pallas_call(
        add_norm_kernel,
        out_shape=[jax.ShapeDtypeStruct(hidden.shape, BF16)] * 2,
        compiler_params=PARAMS,
        cost_estimate=pl.CostEstimate(flops=4000000, bytes_accessed=10 * hidden.size, transcendentals=0),
        name="add_norm",
    )(hidden, here, there, gain)


def finish_kernel(mine_ref, *refs):
    *ins, out_ref = refs
    half = out_ref.shape[2] // 2
    first = mine_ref[0] == 0
    for c in range(out_ref.shape[0]):
        hidden_ref, own_ref, oth_ref = ins[3 * c:3 * c + 3]
        own = (hidden_ref[0].astype(F32) + own_ref[...].astype(F32)).astype(BF16)
        oth = (hidden_ref[1].astype(F32) + oth_ref[...].astype(F32)).astype(BF16)
        out_ref[c, :, :half] = jnp.where(first, own, oth)
        out_ref[c, :, half:] = jnp.where(first, oth, own)


def finish(mine, ins, shape):
    return pl.pallas_call(
        finish_kernel,
        in_specs=[pl.BlockSpec(memory_space=pltpu.SMEM)] + [pl.BlockSpec(memory_space=pltpu.VMEM)] * len(ins),
        out_shape=jax.ShapeDtypeStruct(shape, BF16),
        compiler_params=PARAMS,
        name="finish",
    )(mine, *ins)


def qkv_kernel(flip, idx_ref, h_ref, q_own, q_oth, kv_own, kv_oth, q_ref, kv_ref):
    h_a, h_b = (h_ref[1], h_ref[0]) if flip else (h_ref[0], h_ref[1])
    for own, oth, out in ((q_own, q_oth, q_ref), (kv_own, kv_oth, kv_ref)):
        total = jnp.dot(h_a, own[...], preferred_element_type=F32) + jnp.dot(h_b, oth[...], preferred_element_type=F32)
        out[...] = total.astype(BF16)


def qkv(h, flip, w_in, q_oth, w_kv, kv_oth, layer, idx, tile_m=512):
    _, rows, half = h.shape
    n_q, n_kv = q_oth.shape[1], w_kv.shape[2]
    return pl.pallas_call(
        functools.partial(qkv_kernel, flip),
        grid_spec=pltpu.PrefetchScalarGridSpec(
            num_scalar_prefetch=1,
            grid=(rows // tile_m,),
            in_specs=[
                pl.BlockSpec((2, tile_m, half), lambda m, s: (0, m, 0)),
                pl.BlockSpec((None, half, n_q), lambda m, s: (layer, 0, s[0])),
                pl.BlockSpec((half, n_q), lambda m, s: (0, 0)),
                pl.BlockSpec((None, half, n_kv), lambda m, s: (layer, 0, 0)),
                pl.BlockSpec((None, half, n_kv), lambda m, s: (layer, 0, 0)),
            ],
            out_specs=[pl.BlockSpec((tile_m, n_q), lambda m, s: (m, 0)), pl.BlockSpec((tile_m, n_kv), lambda m, s: (m, 0))],
        ),
        out_shape=[jax.ShapeDtypeStruct((rows, n_q), BF16), jax.ShapeDtypeStruct((rows, n_kv), BF16)],
        compiler_params=PARAMS,
        cost_estimate=pl.CostEstimate(flops=4 * rows * half * (n_q + n_kv), bytes_accessed=4 * rows * half + 4 * half * (n_q + n_kv), transcendentals=0),
        name="qkv",
    )(idx, h, w_in, q_oth, w_kv, kv_oth)


def gated_kernel(flip, idx_ref, h_ref, g_own, u_own, g_oth, u_oth, out_ref):
    h_a, h_b = (h_ref[1], h_ref[0]) if flip else (h_ref[0], h_ref[1])
    gate = jnp.dot(h_a, g_own[...], preferred_element_type=F32) + jnp.dot(h_b, g_oth[...], preferred_element_type=F32)
    up = jnp.dot(h_a, u_own[...], preferred_element_type=F32) + jnp.dot(h_b, u_oth[...], preferred_element_type=F32)
    gate = gate.astype(BF16).astype(F32)
    up = up.astype(BF16).astype(F32)
    out_ref[...] = (gate * jax.nn.sigmoid(gate) * up).astype(BF16)


def gated(h, flip, w_in, g_oth, u_oth, layer, idx, g_col, u_col, tile_m=1024, tile_n=512):
    _, rows, half = h.shape
    width = g_oth.shape[1]
    n_tiles = width // tile_n
    g_blk, u_blk = g_col // tile_n, u_col // tile_n
    return pl.pallas_call(
        functools.partial(gated_kernel, flip),
        grid_spec=pltpu.PrefetchScalarGridSpec(
            num_scalar_prefetch=1,
            grid=(n_tiles, rows // tile_m),
            in_specs=[
                pl.BlockSpec((2, tile_m, half), lambda n, m, s: (0, m, 0)),
                pl.BlockSpec((None, half, tile_n), lambda n, m, s: (layer, 0, g_blk + s[0] + n)),
                pl.BlockSpec((None, half, tile_n), lambda n, m, s: (layer, 0, u_blk + s[0] + n)),
                pl.BlockSpec((half, tile_n), lambda n, m, s: (0, n)),
                pl.BlockSpec((half, tile_n), lambda n, m, s: (0, n)),
            ],
            out_specs=pl.BlockSpec((tile_m, tile_n), lambda n, m, s: (m, n)),
        ),
        out_shape=jax.ShapeDtypeStruct((rows, width), BF16),
        compiler_params=PARAMS,
        cost_estimate=pl.CostEstimate(flops=8 * rows * half * width, bytes_accessed=4 * rows * half * n_tiles + 8 * half * width + 2 * rows * width, transcendentals=rows * width),
        name="gated",
    )(idx, h, w_in, w_in, g_oth, u_oth)


def project_kernel(n_lhs, set_sizes, *refs):
    lhs, out_ref = refs[:n_lhs], refs[-1]
    start = n_lhs
    for k, size in enumerate(set_sizes):
        weights = refs[start:start + size]
        start += size
        pos, row, acc = 0, 0, None
        for ref in lhs:
            depth = ref.shape[1]
            if row == weights[pos].shape[0]:
                pos, row = pos + 1, 0
            part = jnp.dot(ref[...], weights[pos][row:row + depth, :], preferred_element_type=F32)
            acc = part if acc is None else acc + part
            row += depth
        out_ref[k] = acc.astype(BF16)


def project(lhs, sets, layer=None, tile_m=1024, tile_n=512):
    rows = lhs[0].shape[0]
    depth = sum(a.shape[1] for a in lhs)
    cols = sets[0][0].shape[-1]
    specs = []
    for weights in sets:
        for w in weights:
            if layer is None:
                specs.append(pl.BlockSpec((w.shape[0], tile_n), lambda n, m: (0, n)))
            else:
                specs.append(pl.BlockSpec((None, w.shape[1], tile_n), lambda n, m: (layer, 0, n)))
    return pl.pallas_call(
        functools.partial(project_kernel, len(lhs), [len(weights) for weights in sets]),
        grid=(cols // tile_n, rows // tile_m),
        in_specs=[pl.BlockSpec((tile_m, a.shape[1]), lambda n, m: (m, 0)) for a in lhs] + specs,
        out_specs=pl.BlockSpec((len(sets), tile_m, tile_n), lambda n, m: (0, m, n)),
        out_shape=jax.ShapeDtypeStruct((len(sets), rows, cols), BF16),
        compiler_params=PARAMS,
        cost_estimate=pl.CostEstimate(flops=2 * rows * depth * cols * len(sets), bytes_accessed=2 * (rows * depth * (cols // tile_n) + depth * cols * len(sets) + rows * cols * len(sets)), transcendentals=0),
        name="project",
    )(*lhs, *[w for weights in sets for w in weights])


def attend_kernel(block, n_blocks, which_seq, lens_ref, q_ref, k_ref, v_ref, out_ref):
    seq_len = lens_ref[which_seq]
    which = pl.program_id(1)
    head_dim = q_ref.shape[1]
    for blk in range(n_blocks):
        @pl.when(which == blk)
        def _(blk=blk):
            keys = (blk + 1) * block
            scores = lax.dot_general(q_ref[...], k_ref[:keys, :], (((1,), (1,)), ((), ())), preferred_element_type=F32) * (head_dim ** -0.5)
            key_pos = lax.broadcasted_iota(jnp.int32, (block, keys), 1)
            q_pos = blk * block + lax.broadcasted_iota(jnp.int32, (block, keys), 0)
            scores = jnp.where((key_pos <= q_pos) & (key_pos < seq_len), scores, -1e30)
            top = jnp.max(scores, axis=-1, keepdims=True)
            weights = jnp.exp(scores - top)
            probs = (weights / jnp.sum(weights, axis=-1, keepdims=True)).astype(BF16)
            out_ref[...] = jnp.dot(probs, v_ref[:keys, :], preferred_element_type=F32).astype(BF16)


def attend(q, kv, lens, which_seq, block=512):
    length, width = q.shape
    head_dim = kv.shape[1] // 2
    n_heads, n_blocks = width // head_dim, length // block
    return pl.pallas_call(
        functools.partial(attend_kernel, block, n_blocks, which_seq),
        grid_spec=pltpu.PrefetchScalarGridSpec(
            num_scalar_prefetch=1,
            grid=(n_heads, n_blocks),
            in_specs=[
                pl.BlockSpec((block, head_dim), lambda i, b, s: (b, i)),
                pl.BlockSpec((length, head_dim), lambda i, b, s: (0, 0)),
                pl.BlockSpec((length, head_dim), lambda i, b, s: (0, 1)),
            ],
            out_specs=pl.BlockSpec((block, head_dim), lambda i, b, s: (b, i)),
        ),
        out_shape=jax.ShapeDtypeStruct((length, width), BF16),
        compiler_params=PARAMS,
        cost_estimate=pl.CostEstimate(flops=4 * n_heads * length * length * head_dim * 5 // 8, bytes_accessed=8 * length * width, transcendentals=n_heads * length * length),
        name="attend",
    )(lens, q, kv, kv)


def solution(mesh):
    batch_axes = ("rep", "data")
    n_model = mesh.shape["model"]
    swap = [(0, 1), (1, 0)]
    in0 = (1024, 1024)
    in1 = (1024, 512, 512, 1024, 1024)

    def across(value):
        return lax.ppermute(value, "data", swap)

    def gather(value):
        return lax.all_gather(value, "model", axis=1, tiled=True)

    def scatter(value):
        return lax.psum_scatter(value, "model", scatter_dimension=1, tiled=True)

    def local_body(x_loc, lens_loc, gamma_loc, w_in_loc, w_kv_loc, w_out_loc):
        half = gamma_loc.shape[1]
        kv_cols = w_kv_loc.shape[2]
        out_local = w_out_loc.shape[1]
        ff = w_in_loc.shape[2] - out_local
        attn_cols = out_local - ff
        b_q, b_ff = attn_cols // 2, ff // 2
        mine = lax.axis_index("data")
        theirs = 1 - mine
        slot = lax.axis_index("model")
        mine_arr = mine.astype(jnp.int32).reshape(1)
        shift = mine_arr * (b_ff // 512)
        none = jnp.zeros((1,), jnp.int32)

        def cols(start, width):
            return lax.dynamic_slice(w_in_loc, (0, 0, start), (1, half, width))[0]

        def out_rows(which):
            return [
                lax.dynamic_slice(w_out_loc, (0, which * b_q, 0), (1, b_q, half))[0],
                lax.dynamic_slice(w_out_loc, (0, attn_cols + which * b_ff, 0), (1, b_ff, half))[0],
            ]

        def gain(layer):
            return jnp.stack([gamma_loc[layer], gamma_oth[layer]])

        gamma_oth = across(gamma_loc)
        lens_oth = across(lens_loc)
        part = half // n_model
        kv_oth = gather(across(lax.dynamic_slice(w_kv_loc, (0, slot * part, 0), (2, part, kv_cols))))

        q0_oth = across(cols(theirs * b_q, b_q))
        in0_oth = []
        at = attn_cols + theirs * b_ff
        for width in in0:
            in0_oth.append((across(cols(at, width)), across(cols(ff + at, width))))
            at += width
        hidden, normed = [], []
        for c in range(2):
            x_c, n_c = first_norm(mine_arr, x_loc, gain(0), c)
            hidden.append(x_c)
            normed.append(n_c)
        h0_oth = [across(normed[c]) for c in range(2)]
        top, low = out_rows(theirs)
        out0_oth = [across(top), across(low)]
        q1_oth = across(w_in_loc[1, :, :attn_cols])
        in1_oth = []
        at = attn_cols
        for width in in1:
            in1_oth.append((across(w_in_loc[1, :, at:at + width]), across(w_in_loc[1, :, ff + at:ff + at + width])))
            at += width
        out1_oth = across(w_out_loc[1])

        lhs0 = {}
        for name, flip, tokens, lens, which in (("o0", False, normed[0], lens_loc, 0), ("o1", False, normed[1], lens_loc, 1), ("p0", True, h0_oth[0], lens_oth, 0), ("p1", True, h0_oth[1], lens_oth, 1)):
            h = gather(tokens)
            q, kv = qkv(h, flip, w_in_loc, q0_oth, w_kv_loc, kv_oth, 0, mine_arr)
            lhs = [attend(q, kv, lens, which)]
            at = attn_cols
            for c, width in enumerate(in0):
                lhs.append(gated(h, flip, w_in_loc, *in0_oth[c], 0, shift, at, ff + at))
                at += width
            lhs0[name] = lhs
        own_sets = out_rows(mine)
        z0 = {}
        for name, lhs in lhs0.items():
            z = project(lhs, [own_sets, out0_oth])
            z0[name] = scatter(z)
        z_got = [across(z0[f"p{c}"]) for c in range(2)]

        ends = []
        for c in range(2):
            x_c, n_c = add_norm(hidden[c], z0[f"o{c}"], z_got[c], gain(1))
            h = gather(n_c)
            q, kv = qkv(h, False, w_in_loc, q1_oth, w_kv_loc, kv_oth, 1, none)
            lhs = [attend(q, kv, lens_loc, c)]
            at = attn_cols
            for k, width in enumerate(in1):
                lhs.append(gated(h, False, w_in_loc, *in1_oth[k], 1, none, at, ff + at))
                at += width
            z_own = project(lhs, [[w_out_loc]], layer=1)
            z_oth = project(lhs, [[out1_oth]])
            ends += [x_c, scatter(z_own)[0], scatter(z_oth)[0]]
        return finish(mine_arr, ends, x_loc.shape)

    in_specs = (
        P(batch_axes, "model", None),
        P(batch_axes),
        P(None, "data"),
        P(None, "data", "model"),
        P(None, "data", None),
        P(None, "model", "data"),
    )
    return jax.shard_map(local_body, mesh=mesh, in_specs=in_specs, out_specs=P(batch_axes, "model", None), check_vma=False)
```

time: 2330 us -> 1770 us (0.76)
  Pallas kernels: 0 us -> 769 us
  matrix products: 697 us -> 0 us
  waiting for transfers between devices: 1220 us -> 906 us
  other arithmetic: 206 us -> 1.2 us
  local copies, waits for them, and re-layouts: 158 us -> 52.5 us
  starting transfers between devices: 0.37 us -> 27.9 us
    all_gather x8 -> x7, waiting for transfers between devices: 984 us -> 0.08 us  [gather(): return lax.all_gather(value, 'model', axis=1, tiled=True)]
    ppermute x0 -> x26, waiting for transfers between devices: none -> 828 us  [across(): return lax.ppermute(value, 'data', swap)]
    pallas_call x0 -> x43, Pallas kernels: none -> 769 us  [the longest x18 377 us: gated(): pl.pallas_call(functools.partial(gated_kernel, flip), grid_spec=pltpu.Pre...]
    dot_general x24 -> x0, matrix products: 697 us -> none  [the longest x2 320 us: local_step(): jnp.einsum('btd,dc->btc', h_full, w_in_full, preferred_element_type=jnp.f...]
    sub x8 -> x0, other arithmetic: 163 us -> none  [one_block(): attn_probs = jax.nn.softmax(scores, axis=-1).astype(jnp.bfloat16)]
    reduce_scatter x2 -> x8, waiting for transfers between devices: 233 us -> 76.5 us  [scatter(): return lax.psum_scatter(value, 'model', scatter_dimension=1, tiled=True)]
    slice x8 -> x2, local copies, waits for them, and re-layouts: 57.2 us -> 1.95 us  [gain(): return jnp.stack([gamma_loc[layer], gamma_oth[layer]])]
    transpose x2 -> x0, local copies, waits for them, and re-layouts: 46 us -> none  [local_step(): jnp.einsum('nbqe,ed->bnqd', attn_blocks, w_out_full[:attn_cols], preferre...]
  transfers between devices with their start and end apart: 10 -> 41, of which waited for: 6 -> 22; matrix products, arithmetic and copies ran while one was open for 34% -> 2% of each run, Pallas kernels for 0% -> 43%
where the time goes in v2:
time: 1770 us
  waiting for transfers between devices  906 us (51%)
  Pallas kernels  769 us (43%)
  local copies, waits for them, and re-layouts  52.5 us (3%)
  starting transfers between devices  27.9 us (2%)
    ppermute x26, waiting for transfers between devices, across(): return lax.ppermute(value, 'data', swap)  828 us
    pallas_call x18, Pallas kernels, gated(): pl.pallas_call(functools.partial(gated_kernel, flip), grid_spec=pltpu.Pre...  377 us
    pallas_call x8, Pallas kernels, project(): pl.pallas_call(functools.partial(project_kernel, len(lhs), [len(weights)...  210 us
    pallas_call x6, Pallas kernels, attend(): pl.pallas_call(functools.partial(attend_kernel, block, n_blocks, which_se...  83.3 us
    reduce_scatter x8, waiting for transfers between devices, scatter(): return lax.psum_scatter(value, 'model', scatter_dimension=1, tiled=True)  76.5 us
    pallas_call x6, Pallas kernels, qkv(): pl.pallas_call(functools.partial(qkv_kernel, flip), grid_spec=pltpu.Prefe...  72.3 us
  transfers between devices with their start and end apart: 41, of which 22 were waited for; matrix products, arithmetic and copies ran while one was open for 2% of the time, Pallas kernels for 43%

profile of v2, /device:TPU:0, one launch (start us, length us, event | category | flops | bytes accessed | tf_op | source)
XLA Modules:
  0.0 1770.2 jit_solution(17885741911533522423)
XLA Ops:
  18.9 44.8 %collective-permute-done.24 = bf16[2,512,1024]{2,1,0:T(8,128)(2,1)S(1)} collective-permute-done((bf16[2,512,1024]{2,1,0:T(8,128)(2,1)}, bf16[2,512,1024]{2,1,0:T(8,128)(2,1)S(1)}, u32[]{:S(2)}, u32[]{:S(2)}) %collective-permute-start.24) | collective-permute-done | bytes 2097184 | tf_op jit(solution)/shard_map/ppermute | solution.py:251
  85.2 44.2 %collective-permute-done.10 = bf16[2,512,1024]{2,1,0:T(8,128)(2,1)S(1)} collective-permute-done((bf16[2,512,1024]{2,1,0:T(8,128)(2,1)}, bf16[2,512,1024]{2,1,0:T(8,128)(2,1)S(1)}, u32[]{:S(2)}, u32[]{:S(2)}) %collective-permute-start.10) | collective-permute-done | bytes 2097184 | tf_op jit(solution)/shard_map/ppermute | solution.py:251
  163.9 31.4 %collective-permute-done.3.g_oth = bf16[1024,1024]{1,0:T(8,128)(2,1)S(1)} collective-permute-done((bf16[1024,1024]{1,0:T(8,128)(2,1)}, bf16[1024,1024]{1,0:T(8,128)(2,1)S(1)}, u32[]{:S(2)}, u32[]{:S(2)}) %collective-permute-start.3) | collective-permute-done | bytes 2097184 | tf_op jit(solution)/shard_map/ppermute | solution.py:251
  195.9 44.5 %collective-permute-done.4.u_oth = bf16[1024,1024]{1,0:T(8,128)(2,1)} collective-permute-done((bf16[1024,1024]{1,0:T(8,128)(2,1)}, bf16[1024,1024]{1,0:T(8,128)(2,1)}, u32[]{:S(2)}, u32[]{:S(2)}) %collective-permute-start.4) | collective-permute-done | bytes 2097184 | tf_op jit(solution)/shard_map/ppermute | solution.py:251
  240.9 23.1 %gated.29.refs_1_ = bf16[2048,1024]{1,0:T(8,128)(2,1)} custom-call(s32[1]{0:T(128)S(6)} %mul.22.idx_ref, bf16[2,2048,1024]{2,1,0:T(8,128)(2,1)} %all-gather.18.cloned.1.call-done.h_ref, bf16[2,1024,8704]{2,1,0:T(8,128)(2,1)} %u_own.35, bf16[2,1024,8704]{2,1,0:T(8,128)(2,1)} %u_own.35, bf16[1024,1024]{1,0:T(8,128)(2,1)} %copy-done, ...), custom_call_target="tpu_custom_call" | custom-call | flops 17179869184 | bytes 29360128 | tf_op jit(solution)/shard_map/gated/pallas_call | solution.py:141
  285.9 44.4 %collective-permute-done.6.u_oth = bf16[1024,1024]{1,0:T(8,128)(2,1)} collective-permute-done((bf16[1024,1024]{1,0:T(8,128)(2,1)}, bf16[1024,1024]{1,0:T(8,128)(2,1)}, u32[]{:S(2)}, u32[]{:S(2)}) %collective-permute-start.6) | collective-permute-done | bytes 2097184 | tf_op jit(solution)/shard_map/ppermute | solution.py:251
  353.1 78.2 %collective-permute-done.1.q_oth = bf16[1024,256]{1,0:T(8,128)(2,1)S(1)} collective-permute-done((bf16[1024,256]{1,0:T(8,128)(2,1)S(1)}, bf16[1024,256]{1,0:T(8,128)(2,1)S(1)}, u32[]{:S(2)}, u32[]{:S(2)}) %collective-permute-start.1) | collective-permute-done | bytes 524320 | tf_op jit(solution)/shard_map/ppermute | solution.py:251
  455.3 25.4 %project.13 = bf16[2,2048,1024]{2,1,0:T(8,128)(2,1)} custom-call(bf16[2048,256]{1,0:T(8,128)(2,1)} %attend.10.refs_0_, bf16[2048,1024]{1,0:T(8,128)(2,1)} %gated.29.refs_1_, bf16[2048,1024]{1,0:T(8,128)(2,1)} %gated.30.refs_2_, bf16[256,1024]{1,0:T(8,128)(2,1)} %get-tuple-element.63.refs_3_, bf16[2048,1024]{1,0:T(8,128)(2,1)} %get-tuple-element.61.refs_4_, ...), custom_call_target="tpu_custom_call" | custom-call | flops 19327352832 | bytes 36700160 | tf_op jit(solution)/shard_map/project/pallas_call | solution.py:190
  549.9 25.5 %project.12 = bf16[2,2048,1024]{2,1,0:T(8,128)(2,1)} custom-call(bf16[2048,256]{1,0:T(8,128)(2,1)} %attend.9.refs_0_, bf16[2048,1024]{1,0:T(8,128)(2,1)} %gated.27.refs_1_, bf16[2048,1024]{1,0:T(8,128)(2,1)} %gated.28.refs_2_, bf16[256,1024]{1,0:T(8,128)(2,1)} %get-tuple-element.63.refs_3_, bf16[2048,1024]{1,0:T(8,128)(2,1)} %get-tuple-element.61.refs_4_, ...), custom_call_target="tpu_custom_call" | custom-call | flops 19327352832 | bytes 36700160 | tf_op jit(solution)/shard_map/project/pallas_call | solution.py:190
  621.1 23.3 %gated.21.refs_2_ = bf16[2048,1024]{1,0:T(8,128)(2,1)} custom-call(s32[1]{0:T(128)S(6)} %mul.22.idx_ref, bf16[2,2048,1024]{2,1,0:T(8,128)(2,1)} %all-gather.12.cloned.1.call-done.h_ref, bf16[2,1024,8704]{2,1,0:T(8,128)(2,1)} %u_own.35, bf16[2,1024,8704]{2,1,0:T(8,128)(2,1)} %u_own.35, bf16[1024,1024]{1,0:T(8,128)(2,1)} %collective-permute-done.5.g_oth, ...), custom_call_target="tpu_custom_call" | custom-call | flops 17179869184 | bytes 29360128 | tf_op jit(solution)/shard_map/gated/pallas_call | solution.py:141
  644.5 25.5 %project.9 = bf16[2,2048,1024]{2,1,0:T(8,128)(2,1)} custom-call(bf16[2048,256]{1,0:T(8,128)(2,1)} %attend.7.refs_0_, bf16[2048,1024]{1,0:T(8,128)(2,1)} %gated.20.refs_1_, bf16[2048,1024]{1,0:T(8,128)(2,1)} %gated.21.refs_2_, bf16[256,1024]{1,0:T(8,128)(2,1)} %get-tuple-element.63.refs_3_, bf16[2048,1024]{1,0:T(8,128)(2,1)} %get-tuple-element.61.refs_4_, ...), custom_call_target="tpu_custom_call" | custom-call | flops 19327352832 | bytes 36700160 | tf_op jit(solution)/shard_map/project/pallas_call | solution.py:190
  715.9 23.3 %gated.18.refs_1_ = bf16[2048,1024]{1,0:T(8,128)(2,1)} custom-call(s32[1]{0:T(128)S(6)} %mul.22.idx_ref, bf16[2,2048,1024]{2,1,0:T(8,128)(2,1)} %all-gather.8.cloned.1.call-done.h_ref, bf16[2,1024,8704]{2,1,0:T(8,128)(2,1)} %u_own.35, bf16[2,1024,8704]{2,1,0:T(8,128)(2,1)} %u_own.35, bf16[1024,1024]{1,0:T(8,128)(2,1)} %copy-done, ...), custom_call_target="tpu_custom_call" | custom-call | flops 17179869184 | bytes 29360128 | tf_op jit(solution)/shard_map/gated/pallas_call | solution.py:141
  739.2 25.5 %project.8 = bf16[2,2048,1024]{2,1,0:T(8,128)(2,1)} custom-call(bf16[2048,256]{1,0:T(8,128)(2,1)} %attend.6.refs_0_, bf16[2048,1024]{1,0:T(8,128)(2,1)} %gated.18.refs_1_, bf16[2048,1024]{1,0:T(8,128)(2,1)} %gated.19.refs_2_, bf16[256,1024]{1,0:T(8,128)(2,1)} %get-tuple-element.63.refs_3_, bf16[2048,1024]{1,0:T(8,128)(2,1)} %get-tuple-element.61.refs_4_, ...), custom_call_target="tpu_custom_call" | custom-call | flops 19327352832 | bytes 36700160 | tf_op jit(solution)/shard_map/project/pallas_call | solution.py:190
  766.0 36.9 %collective-permute-done.25.there_ref = bf16[2,512,1024]{2,1,0:T(8,128)(2,1)S(1)} collective-permute-done((bf16[2,512,1024]{2,1,0:T(8,128)(2,1)}, bf16[2,512,1024]{2,1,0:T(8,128)(2,1)S(1)}, u32[]{:S(2)}, u32[]{:S(2)}) %collective-permute-start.25) | collective-permute-done | bytes 2097184 | tf_op jit(solution)/shard_map/ppermute | solution.py:251
  872.0 219.0 %collective-permute-done.17.g_oth = bf16[1024,512]{1,0:T(8,128)(2,1)S(1)} collective-permute-done((bf16[1024,512]{1,0:T(8,128)(2,1)S(1)}, bf16[1024,512]{1,0:T(8,128)(2,1)S(1)}, u32[]{:S(2)}, u32[]{:S(2)}) %collective-permute-start.17) | collective-permute-done | bytes 1048608 | tf_op jit(solution)/shard_map/ppermute | solution.py:251
  1164.0 84.4 %collective-permute-done.15.g_oth = bf16[1024,512]{1,0:T(8,128)(2,1)} collective-permute-done((bf16[1024,512]{1,0:T(8,128)(2,1)}, bf16[1024,512]{1,0:T(8,128)(2,1)}, u32[]{:S(2)}, u32[]{:S(2)}) %collective-permute-start.15) | collective-permute-done | bytes 1048608 | tf_op jit(solution)/shard_map/ppermute | solution.py:251
  1287.5 23.1 %gated.35.refs_5_ = bf16[2048,1024]{1,0:T(8,128)(2,1)} custom-call(s32[1]{0:T(128)} %constant.46.clone.1.idx_ref, bf16[2,2048,1024]{2,1,0:T(8,128)(2,1)} %all-gather.20.cloned.1.call-done.h_ref, bf16[2,1024,8704]{2,1,0:T(8,128)(2,1)} %u_own.35, bf16[2,1024,8704]{2,1,0:T(8,128)(2,1)} %u_own.35, bf16[1024,1024]{1,0:T(8,128)(2,1)} %copy-done.2, ...), custom_call_target="tpu_custom_call" | custom-call | flops 17179869184 | bytes 29360128 | tf_op jit(solution)/shard_map/gated/pallas_call | solution.py:141
  1330.3 30.4 %collective-permute-done.20.u_oth = bf16[1024,1024]{1,0:T(8,128)(2,1)} collective-permute-done((bf16[1024,1024]{1,0:T(8,128)(2,1)}, bf16[1024,1024]{1,0:T(8,128)(2,1)}, u32[]{:S(2)}, u32[]{:S(2)}) %collective-permute-start.20) | collective-permute-done | bytes 2097184 | tf_op jit(solution)/shard_map/ppermute | solution.py:251
  1405.7 33.4 %collective-permute-done.14.u_oth = bf16[1024,1024]{1,0:T(8,128)(2,1)} collective-permute-done((bf16[1024,1024]{1,0:T(8,128)(2,1)}, bf16[1024,1024]{1,0:T(8,128)(2,1)}, u32[]{:S(2)}, u32[]{:S(2)}) %collective-permute-start.14) | collective-permute-done | bytes 2097184 | tf_op jit(solution)/shard_map/ppermute | solution.py:251
  1462.0 27.0 %project.15 = bf16[1,2048,1024]{2,1,0:T(8,128)(2,1)} custom-call(bf16[2048,512]{1,0:T(8,128)(2,1)} %attend.11.refs_0_, bf16[2048,1024]{1,0:T(8,128)(2,1)} %gated.31.refs_1_, bf16[2048,512]{1,0:T(8,128)(2,1)} %gated.32.refs_2_, bf16[2048,512]{1,0:T(8,128)(2,1)} %gated.33.refs_3_, bf16[2048,1024]{1,0:T(8,128)(2,1)} %gated.34.refs_4_, ...), custom_call_target="tpu_custom_call" | custom-call | flops 19327352832 | bytes 51380224 | tf_op jit(solution)/shard_map/project/pallas_call | solution.py:190
  1489.1 27.0 %project.14 = bf16[1,2048,1024]{2,1,0:T(8,128)(2,1)} custom-call(bf16[2048,512]{1,0:T(8,128)(2,1)} %attend.11.refs_0_, bf16[2048,1024]{1,0:T(8,128)(2,1)} %gated.31.refs_1_, bf16[2048,512]{1,0:T(8,128)(2,1)} %gated.32.refs_2_, bf16[2048,512]{1,0:T(8,128)(2,1)} %gated.33.refs_3_, bf16[2048,1024]{1,0:T(8,128)(2,1)} %gated.34.refs_4_, ...), custom_call_target="tpu_custom_call" | custom-call | flops 19327352832 | bytes 51380224 | tf_op jit(solution)/shard_map/project/pallas_call | solution.py:190
  1644.7 27.0 %project.11 = bf16[1,2048,1024]{2,1,0:T(8,128)(2,1)} custom-call(bf16[2048,512]{1,0:T(8,128)(2,1)} %attend.8.refs_0_, bf16[2048,1024]{1,0:T(8,128)(2,1)} %gated.22.refs_1_, bf16[2048,512]{1,0:T(8,128)(2,1)} %gated.23.refs_2_, bf16[2048,512]{1,0:T(8,128)(2,1)} %gated.24.refs_3_, bf16[2048,1024]{1,0:T(8,128)(2,1)} %gated.25.refs_4_, ...), custom_call_target="tpu_custom_call" | custom-call | flops 19327352832 | bytes 51380224 | tf_op jit(solution)/shard_map/project/pallas_call | solution.py:190
  1671.9 27.2 %project.10 = bf16[1,2048,1024]{2,1,0:T(8,128)(2,1)} custom-call(bf16[2048,512]{1,0:T(8,128)(2,1)} %attend.8.refs_0_, bf16[2048,1024]{1,0:T(8,128)(2,1)} %gated.22.refs_1_, bf16[2048,512]{1,0:T(8,128)(2,1)} %gated.23.refs_2_, bf16[2048,512]{1,0:T(8,128)(2,1)} %gated.24.refs_3_, bf16[2048,1024]{1,0:T(8,128)(2,1)} %gated.25.refs_4_, ...), custom_call_target="tpu_custom_call" | custom-call | flops 19327352832 | bytes 51380224 | tf_op jit(solution)/shard_map/project/pallas_call | solution.py:190
  1715.3 41.4 %reduce-scatter.13.cloned.1.call-done = bf16[1,512,1024]{2,1,0:T(8,128)(2,1)} async-done(((bf16[1,2048,1024]{2,1,0:T(8,128)(2,1)}), bf16[1,512,1024]{2,1,0:T(8,128)(2,1)}) %reduce-scatter.13.cloned.1.call-update) | async-done | bytes 1048592 | tf_op jit(solution)/shard_map/reduce_scatter | solution.py:257
  (155 shorter events, 720.4 us)
Async XLA Ops:
  6.5 234.4 %all-gather.18.cloned.1.call-start = ((), (), s32[]{:S(2)}) async-start(), calls=%async_computation.18 | async-start | bytes 10485760 | tf_op jit(solution)/shard_map/all_gather | solution.py:254
  65.1 366.2 %all-gather.10.cloned.1.call-start = ((), (), s32[]{:S(2)}) async-start(), calls=%async_computation.9 | async-start | bytes 2621440 | tf_op jit(solution)/shard_map/all_gather | solution.py:254
  79.2 401.5 %all-gather.16.cloned.1.call-start = ((), (), s32[]{:S(2)}) async-start(), calls=%async_computation.16 | async-start | bytes 10485760 | tf_op jit(solution)/shard_map/all_gather | solution.py:254
  80.0 495.5 %all-gather.12.cloned.1.call-start = ((), (), s32[]{:S(2)}) async-start(), calls=%async_computation.11 | async-start | bytes 10485760 | tf_op jit(solution)/shard_map/all_gather | solution.py:254
  130.7 539.3 %all-gather.8.cloned.1.call-start = ((), (), s32[]{:S(2)}) async-start(), calls=%async_computation.8 | async-start | bytes 10485760 | tf_op jit(solution)/shard_map/all_gather | solution.py:254
  131.3 633.5 %reduce-scatter.19.cloned.1.call-start = ((), (), s32[]{:S(2)}) async-start(), calls=%async_computation.19 | async-start | bytes 10485760 | tf_op jit(solution)/shard_map/reduce_scatter | solution.py:257
  149.2 181.1 %collective-permute-start.6 = (bf16[1024,1024]{1,0:T(8,128)(2,1)}, bf16[1024,1024]{1,0:T(8,128)(2,1)}, u32[]{:S(2)}, u32[]{:S(2)}) collective-permute-start(bf16[1024,1024]{1,0:T(8,128)(2,1)} %get-tuple-element.51), channel_id=1, source_target_pairs={{0,4},{4,0},{1,5},{5,1},{2,6},{6,2},{3,7},{7,3}} | collective-permute-start | bytes 6291464 | tf_op jit(solution)/shard_map/ppermute | solution.py:251
  160.1 294.4 %collective-permute-start.8 = (bf16[2048,1024]{1,0:T(8,128)(2,1)}, bf16[2048,1024]{1,0:T(8,128)(2,1)}, u32[]{:S(2)}, u32[]{:S(2)}) collective-permute-start(bf16[2048,1024]{1,0:T(8,128)(2,1)} %get-tuple-element.60), channel_id=1, source_target_pairs={{0,4},{4,0},{1,5},{5,1},{2,6},{6,2},{3,7},{7,3}} | collective-permute-start | bytes 12582920 | tf_op jit(solution)/shard_map/ppermute | solution.py:251
  195.3 235.9 %collective-permute-start.1 = (bf16[1024,256]{1,0:T(8,128)(2,1)S(1)}, bf16[1024,256]{1,0:T(8,128)(2,1)S(1)}, u32[]{:S(2)}, u32[]{:S(2)}) collective-permute-start(bf16[1024,256]{1,0:T(8,128)(2,1)S(1)} %dynamic-slice_bitcast_fusion.8), channel_id=1, source_target_pairs={{0,4},{4,0},{1,5},{5,1},{2,6},{6,2},{3,7},{7,3}} | collective-permute-start | bytes 1572872 | tf_op jit(solution)/shard_map/ppermute | solution.py:251
  240.4 202.3 %collective-permute-start.9 = (s32[2]{0:T(128)S(1)}, s32[2]{0:T(128)S(1)}, u32[]{:S(2)}, u32[]{:S(2)}) collective-permute-start(s32[2]{0:T(128)S(1)} %copy-done.12), channel_id=1, source_target_pairs={{0,4},{4,0},{1,5},{5,1},{2,6},{6,2},{3,7},{7,3}} | collective-permute-start | bytes 32 | tf_op jit(solution)/shard_map/ppermute | solution.py:251
  285.3 169.1 %collective-permute-start.7 = (bf16[256,1024]{1,0:T(8,128)(2,1)}, bf16[256,1024]{1,0:T(8,128)(2,1)S(1)}, u32[]{:S(2)}, u32[]{:S(2)}) collective-permute-start(bf16[256,1024]{1,0:T(8,128)(2,1)} %get-tuple-element.62), channel_id=1, source_target_pairs={{0,4},{4,0},{1,5},{5,1},{2,6},{6,2},{3,7},{7,3}} | collective-permute-start | bytes 1572872 | tf_op jit(solution)/shard_map/ppermute | solution.py:251
  480.7 285.3 %reduce-scatter.17.cloned.1.call-start = ((), (), s32[]{:S(2)}) async-start(), calls=%async_computation.17 | async-start | bytes 10485760 | tf_op jit(solution)/shard_map/reduce_scatter | solution.py:257
  575.4 234.7 %reduce-scatter.11.cloned.1.call-start = ((), (), s32[]{:S(2)}) async-start(), calls=%async_computation.12 | async-start | bytes 10485760 | tf_op jit(solution)/shard_map/reduce_scatter | solution.py:257
  764.7 372.4 %all-gather.20.cloned.1.call-start = ((), (), s32[]{:S(2)}) async-start(), calls=%async_computation.20 | async-start | bytes 10485760 | tf_op jit(solution)/shard_map/all_gather | solution.py:254
  810.0 706.1 %all-gather.14.cloned.1.call-start = ((), (), s32[]{:S(2)}) async-start(), calls=%async_computation.13 | async-start | bytes 10485760 | tf_op jit(solution)/shard_map/all_gather | solution.py:254
  854.0 845.1 %reduce-scatter.23.cloned.1.call-start = ((), (), s32[]{:S(2)}) async-start(), calls=%async_computation.22 | async-start | bytes 5242880 | tf_op jit(solution)/shard_map/reduce_scatter | solution.py:257
  862.5 599.5 %collective-permute-start.23 = (bf16[4608,1024]{1,0:T(8,128)(2,1)}, bf16[4608,1024]{1,0:T(8,128)(2,1)}, u32[]{:S(2)}, u32[]{:S(2)}) collective-permute-start(bf16[4608,1024]{1,0:T(8,128)(2,1)} %slice_bitcast_fusion), channel_id=1, source_target_pairs={{0,4},{4,0},{1,5},{5,1},{2,6},{6,2},{3,7},{7,3}} | collective-permute-start | bytes 28311560 | tf_op jit(solution)/shard_map/ppermute | solution.py:251
  867.9 223.0 %collective-permute-start.17 = (bf16[1024,512]{1,0:T(8,128)(2,1)S(1)}, bf16[1024,512]{1,0:T(8,128)(2,1)S(1)}, u32[]{:S(2)}, u32[]{:S(2)}) collective-permute-start(bf16[1024,512]{1,0:T(8,128)(2,1)S(1)} %get-tuple-element.56), channel_id=1, source_target_pairs={{0,4},{4,0},{1,5},{5,1},{2,6},{6,2},{3,7},{7,3}} | collective-permute-start | bytes 3145736 | tf_op jit(solution)/shard_map/ppermute | solution.py:251
  868.9 244.6 %collective-permute-start.18 = (bf16[1024,512]{1,0:T(8,128)(2,1)S(1)}, bf16[1024,512]{1,0:T(8,128)(2,1)}, u32[]{:S(2)}, u32[]{:S(2)}) collective-permute-start(bf16[1024,512]{1,0:T(8,128)(2,1)S(1)} %get-tuple-element.55), channel_id=1, source_target_pairs={{0,4},{4,0},{1,5},{5,1},{2,6},{6,2},{3,7},{7,3}} | collective-permute-start | bytes 3145736 | tf_op jit(solution)/shard_map/ppermute | solution.py:251
  870.0 266.0 %collective-permute-start.12 = (bf16[1024,512]{1,0:T(8,128)(2,1)S(1)}, bf16[1024,512]{1,0:T(8,128)(2,1)}, u32[]{:S(2)}, u32[]{:S(2)}) collective-permute-start(bf16[1024,512]{1,0:T(8,128)(2,1)S(1)} %get-tuple-element.59), channel_id=1, source_target_pairs={{0,4},{4,0},{1,5},{5,1},{2,6},{6,2},{3,7},{7,3}} | collective-permute-start | bytes 3145736 | tf_op jit(solution)/shard_map/ppermute | solution.py:251
  870.9 414.5 %collective-permute-start.21 = (bf16[1024,1024]{1,0:T(8,128)(2,1)}, bf16[1024,1024]{1,0:T(8,128)(2,1)S(1)}, u32[]{:S(2)}, u32[]{:S(2)}) collective-permute-start(bf16[1024,1024]{1,0:T(8,128)(2,1)} %get-tuple-element.46), channel_id=1, source_target_pairs={{0,4},{4,0},{1,5},{5,1},{2,6},{6,2},{3,7},{7,3}} | collective-permute-start | bytes 6291464 | tf_op jit(solution)/shard_map/ppermute | solution.py:251
  1091.0 195.5 %collective-permute-start.22 = (bf16[1024,1024]{1,0:T(8,128)(2,1)}, bf16[1024,1024]{1,0:T(8,128)(2,1)}, u32[]{:S(2)}, u32[]{:S(2)}) collective-permute-start(bf16[1024,1024]{1,0:T(8,128)(2,1)} %get-tuple-element.45), channel_id=1, source_target_pairs={{0,4},{4,0},{1,5},{5,1},{2,6},{6,2},{3,7},{7,3}} | collective-permute-start | bytes 6291464 | tf_op jit(solution)/shard_map/ppermute | solution.py:251
  1489.0 210.1 %reduce-scatter.21.cloned.1.call-start = ((), (), s32[]{:S(2)}) async-start(), calls=%async_computation.21 | async-start | bytes 5242880 | tf_op jit(solution)/shard_map/reduce_scatter | solution.py:257
  1516.0 199.3 %reduce-scatter.15.cloned.1.call-start = ((), (), s32[]{:S(2)}) async-start(), calls=%async_computation.15 | async-start | bytes 5242880 | tf_op jit(solution)/shard_map/reduce_scatter | solution.py:257
  (31 other events, 1618.6 us)
Sparse Core Ops, SparseCore 0:
  65.2 56.5 all-gather.17
  123.3 19.7 all-gather.9
  144.7 55.4 all-gather.15
  201.6 55.4 all-gather.11
  258.5 55.4 all-gather.7
  480.8 66.0 reduce-scatter.18
  575.5 65.5 reduce-scatter.16
  670.1 65.1 reduce-scatter.10
  764.8 64.4 reduce-scatter.8
  830.7 55.4 all-gather.19
  887.8 55.4 all-gather.13
  1489.1 41.9 reduce-scatter.22
  1533.6 39.0 reduce-scatter.20
  1671.9 43.3 reduce-scatter.14
  1717.7 39.0 reduce-scatter.12
